TPU v7x, 256 devices: a whole 4x4x8 slice. The times are simulated.
256 devices in a mesh: ens: 4 (over z_lo, core), gx: 16 (over x, z_hi), gy: 4 (over y).
Axes of the slice: x: 4, y: 4, z: 8 (z_hi: 4, z_lo: 2; z = z_hi * 2 + z_lo), core: 2. Of those that a mesh axis runs over, the one named last changes fastest.
Arguments:
- members: bfloat16 [64, 75, 256, 512], P(('ens', 'gx'), None, None, 'gy'), may hold values from -0.75 to 0.75
- spread: bfloat16 [75, 75], replicated, as said below
- sea_mask: int32 [256, 512], P(('ens', 'gx'), 'gy'), may hold values 0 or 1
- innovations: float32 [75, 256, 512], P(None, ('ens', 'gx'), 'gy'), may hold values from -19 to 19
- obs_error: float32 [75, 256, 512], P(None, ('ens', 'gx'), 'gy'), may hold values from 0.3 to 3
- static_scale: float32 [75, 256, 512], P(None, ('ens', 'gx'), 'gy'), may hold values from 2 to 8
Outputs:
- increment: float32 [75, 256, 512], P(None, ('ens', 'gx'), 'gy')
- alpha_fields: bfloat16 [64, 75, 256, 512], P(('ens', 'gx'), None, None, 'gy')
Inputs may be any that keep to these rules, and one draw needn't show every extreme that they name: `spread`: symmetric and positive definite. `sea_mask`: 1 marks sea, 0 land.
All inputs are finite; a program needn't handle non-finite values. No bound on the sum of `sea_mask` on one device may be relied on, other than what follows from the above.
Results may differ from a plain program's by a relative error of at most 0.0065.
Values may be sent and summed in bfloat16 or wider, within the bound.
No kernel may reach another device: no remote copies, remote signals or barrier semaphores. Data moves between devices by JAX's collectives and lax.ppermute only.
A program may use at most 128 MiB of HBM per device.

v0:
```python
import jax
import jax.numpy as jnp
from jax import lax
from jax.sharding import Mesh
from jax.sharding import PartitionSpec as P

GRIDS = 3
SWEEPS = 2
COARSE_SWEEPS = 4
ITERATIONS = 3
ENS_GX_GY = ("ens_0", "ens_1", "gx_0", "gx_1", "gy")
ENS_GX = ("ens_0", "ens_1", "gx_0", "gx_1")


diffusivity = 16.0
damping = 0.8


def padded_2(x, sides, width):
    edges = {}
    for axis, dim in sides:
        size, length = (lax.axis_size(axis), x.shape[dim])
        up = [(i, (i + 1) % size) for i in range(size - 1)]
        last = lax.slice_in_dim(x, length - width, length, axis=dim)
        leading = lax.slice_in_dim(x, 0, width, axis=dim)
        edges[dim] = (
            lax.ppermute(last, axis, up),
            lax.ppermute(leading, axis, [(b, a) for a, b in up]),
        )
    done = []
    for _, dim in sides:
        low, high = edges[dim]
        around = [(width, width) if d in done else (0, 0) for d in range(x.ndim)]
        x = jnp.concatenate([jnp.pad(low, around), x, jnp.pad(high, around)], axis=dim)
        done.append(dim)
    return x


def by_axis(x, axes):
    for axis in axes:
        x = lax.psum(x, axis)
    return x


def neighbours(padded):
    return padded[:, 2:, 1:-1] + padded[:, :-2, 1:-1] + padded[:, 1:-1, 2:] + padded[:, 1:-1, :-2]


def apply_level(values, strength, padded):
    return values + strength * (4.0 * values - neighbours(padded))


def relax(values, source, strength, padded):
    return values + damping * (source - apply_level(values, strength, padded)) / (
        1.0 + 4.0 * strength
    )


def framed(values):
    return padded_2(values.astype(jnp.bfloat16), ((ENS_GX, 1), ("gy", 2)), 1).astype(values.dtype)


def restrict(values):
    layer_count, row_count, column_count = values.shape
    return 0.25 * values.reshape(layer_count, row_count // 2, 2, column_count // 2, 2).sum(
        axis=(2, 4)
    )


def prolong(values):
    layer_count, row_count, column_count = values.shape
    spread_out = jnp.broadcast_to(
        values[:, :, None, :, None], (layer_count, row_count, 2, column_count, 2)
    )
    return spread_out.reshape(layer_count, 2 * row_count, 2 * column_count)


def coarse_solve(source, strength):
    factor = damping / (1.0 + 4.0 * strength)
    solution = factor * source
    for sweep_index in range(COARSE_SWEEPS - 1):
        padded = padded_2(solution, ((ENS_GX, 1), ("gy", 2)), 1)
        solution = relax(solution, source, strength, padded)
    return solution


def vcycle(source, grid_level):
    strength = diffusivity / 4.0**grid_level
    if grid_level == GRIDS - 1:
        return coarse_solve(source, strength)
    solution = damping / (1.0 + 4.0 * strength) * source
    solution = relax(solution, source, strength, framed(solution))
    remainder = source - apply_level(solution, strength, framed(solution))
    solution = solution + prolong(vcycle(restrict(remainder), grid_level + 1))
    for sweep_index in range(SWEEPS):
        solution = relax(solution, source, strength, framed(solution))
    return solution


def member_products(tiles, spread, masked):
    member_count, layer_count, row_count, column_count = tiles.shape
    product = (tiles * masked).astype(jnp.bfloat16)
    flat = product.reshape(member_count, layer_count, row_count * column_count)
    mixed = jnp.einsum("ij,kjc->kic", spread, flat, preferred_element_type=jnp.float32)
    return mixed.reshape(tiles.shape)


def local(members, spread, sea_mask, innovations, obs_error, static_scale):
    tiles = lax.all_to_all(members, ENS_GX, split_axis=2, concat_axis=0, tiled=True)
    sea = sea_mask.astype(jnp.float32)[None]

    def covariance(direction):
        masked = sea * direction
        mixed = member_products(tiles, spread, masked)
        ensemble = jnp.sum(tiles * mixed, axis=0)
        static = static_scale * vcycle(static_scale * masked, 0)
        return sea * (ensemble + static)

    def system(direction):
        cov_dir = covariance(direction)
        return (cov_dir, cov_dir + obs_error * direction)

    def merged(residual, image):
        return (
            by_axis(jnp.sum(residual * residual), ENS_GX_GY),
            by_axis(jnp.sum(residual * image), ENS_GX_GY),
        )

    weights = jnp.zeros_like(innovations)
    increment = jnp.zeros_like(innovations)
    residual = innovations
    cov_res, image_res = system(residual)
    norm_now, product = merged(residual, image_res)
    alpha = norm_now / product
    direction, along, cov_dir = (residual, image_res, cov_res)
    for iteration in range(ITERATIONS):
        weights = weights + alpha * direction
        increment = increment + alpha * cov_dir
        residual = residual - alpha * along
        if iteration + 1 < ITERATIONS:
            cov_res, image_res = system(residual)
            norm_next, product = merged(residual, image_res)
            ratio = norm_next / norm_now
            alpha = norm_next / (product - ratio * norm_next / alpha)
            direction = residual + ratio * direction
            along = image_res + ratio * along
            cov_dir = cov_res + ratio * cov_dir
            norm_now = norm_next
    final = member_products(tiles, spread, sea * weights).astype(jnp.bfloat16)
    alpha_fields = lax.all_to_all(final, ENS_GX, split_axis=0, concat_axis=2, tiled=True)
    return (increment, alpha_fields)


def solution(mesh):
    split = Mesh(
        mesh.devices.reshape(2, 2, 4, 4, mesh.shape["gy"]), ("ens_0", "ens_1", "gx_0", "gx_1", "gy")
    )
    return jax.shard_map(
        local,
        mesh=split,
        in_specs=(
            P(ENS_GX, None, None, "gy"),
            P(),
            P(ENS_GX, "gy"),
            P(None, ENS_GX, "gy"),
            P(None, ENS_GX, "gy"),
            P(None, ENS_GX, "gy"),
        ),
        out_specs=(P(None, ENS_GX, "gy"), P(ENS_GX, None, None, "gy")),
        check_vma=False,
    )
```

profile of v0, /device:TPU:8, one launch (start us, length us, event | category | flops | bytes accessed | tf_op | source)
XLA Modules:
  0.0 1074.1 jit_solution(13558479619360328652)
XLA Ops:
  0.6 7.9 copy.72
  8.5 12.3 %all-to-all-start = ((bf16[1,75,256,128]{3,1,0,2:T(8,128)(2,1)}), bf16[1,75,256,128]{3,1,0,2:T(8,128)(2,1)}, u32[]{:S(2)}, u32[]{:S(2)}) async-start(bf16[1,75,256,128]{3,1,0,2:T(8,128)(2,1)} %copy.72), calls=%async_computation | async-start | bytes 10485760 | tf_op jit(solution)/shard_map/all_to_all | solution.py:109
  36.0 101.8 %collective-permute-done.2 = bf16[75,1,128]{0,2,1:T(8,128)(2,1)S(1)} collective-permute-done((bf16[75,1,128]{0,2,1:T(8,128)(2,1)S(1)}, bf16[75,1,128]{0,2,1:T(8,128)(2,1)S(1)}, u32[]{:S(2)}, u32[]{:S(2)}) %collective-permute-start.2) | collective-permute-done | bytes 19232 | tf_op jit(solution)/shard_map/ppermute | solution.py:28
  291.7 8.0 collective-permute-start.41
  301.7 8.8 copy.131
  310.5 12.5 %reshape.178 = f32[64,75,512]{2,0,1:T(8,128)} reshape(f32[64,1,75,4,128]{4,3,0,2,1:T(4,128)} %bitcast.87) | data formatting | bytes 19660800 | tf_op jit(solution)/shard_map/convert_element_type | solution.py:115
  329.6 9.0 fusion.2
  341.1 22.1 %all-reduce.80 = (f32[]{:T(128)}, f32[]{:T(128)}) all-reduce(f32[]{:T(128)} %multiply_reduce_fusion.5, f32[]{:T(128)} %get-tuple-element.71), channel_id=1, replica_groups=mesh['ens_0'=2,'ens_1'=2,'gx_0'=4,'gx_1'=4,'gy'=4] {'ens_0'}, use_global_device_ids=true, to_apply=%region_1.2 | all-reduce | flops 2 | bytes 16 | tf_op jit(solution)/shard_map/psum | solution.py:41
  363.1 8.9 all-reduce.77
  372.0 8.3 all-reduce.74
  380.3 11.2 %all-reduce.71 = (f32[]{:T(128)}, f32[]{:T(128)}) all-reduce(f32[]{:T(128)} %get-tuple-element.28, f32[]{:T(128)} %get-tuple-element.29), channel_id=1, replica_groups=mesh['ens_0'=2,'ens_1'=2,'gx_0'=4,'gx_1'=4,'gy'=4] {'gx_1'}, use_global_device_ids=true, to_apply=%region_4.5 | all-reduce | flops 2 | bytes 16 | tf_op jit(solution)/shard_map/psum | solution.py:41
  391.5 9.8 all-reduce.68
  464.1 6.8 collective-permute-start.61
  555.5 8.4 collective-permute-start.81
  580.6 7.6 collective-permute-start.85
  588.1 9.6 fusion.1
  601.6 14.7 %all-reduce.79 = (f32[]{:T(128)}, f32[]{:T(128)}) all-reduce(f32[]{:T(128)} %get-tuple-element.9, f32[]{:T(128)} %get-tuple-element.8), channel_id=1, replica_groups=mesh['ens_0'=2,'ens_1'=2,'gx_0'=4,'gx_1'=4,'gy'=4] {'ens_0'}, use_global_device_ids=true, to_apply=%region_17.18 | all-reduce | flops 2 | bytes 16 | tf_op jit(solution)/shard_map/psum | solution.py:41
  616.3 9.8 all-reduce.76
  626.2 8.3 all-reduce.73
  634.5 17.1 %all-reduce.70 = (f32[]{:T(128)}, f32[]{:T(128)}) all-reduce(f32[]{:T(128)} %get-tuple-element.26, f32[]{:T(128)} %get-tuple-element.27), channel_id=1, replica_groups=mesh['ens_0'=2,'ens_1'=2,'gx_0'=4,'gx_1'=4,'gy'=4] {'gx_1'}, use_global_device_ids=true, to_apply=%region_20.21 | all-reduce | flops 2 | bytes 16 | tf_op jit(solution)/shard_map/psum | solution.py:41
  651.6 9.8 all-reduce.67
  793.7 7.6 collective-permute-start.121
  817.9 8.4 collective-permute-start.125
  843.0 7.6 collective-permute-start.129
  850.6 9.6 fusion
  864.1 16.1 %all-reduce.78 = (f32[]{:T(128)}, f32[]{:T(128)}) all-reduce(f32[]{:T(128)} %get-tuple-element.11, f32[]{:T(128)} %get-tuple-element.10), channel_id=1, replica_groups=mesh['ens_0'=2,'ens_1'=2,'gx_0'=4,'gx_1'=4,'gy'=4] {'ens_0'}, use_global_device_ids=true, to_apply=%region_33.34 | all-reduce | flops 2 | bytes 16 | tf_op jit(solution)/shard_map/psum | solution.py:41
  886.4 8.4 all-reduce.72
  894.8 17.1 %all-reduce.69 = (f32[]{:T(128)}, f32[]{:T(128)}) all-reduce(f32[]{:T(128)} %get-tuple-element.24, f32[]{:T(128)} %get-tuple-element.25), channel_id=1, replica_groups=mesh['ens_0'=2,'ens_1'=2,'gx_0'=4,'gx_1'=4,'gy'=4] {'gx_1'}, use_global_device_ids=true, to_apply=%region_36.37 | all-reduce | flops 2 | bytes 16 | tf_op jit(solution)/shard_map/psum | solution.py:41
  912.0 10.1 all-reduce.66
  939.4 9.3 reshape.181
  955.2 111.1 %all-to-all-done.1 = bf16[64,75,4,128]{3,2,1,0:T(4,128)(2,1)} async-done(((bf16[64,75,4,128]{3,2,1,0:T(4,128)(2,1)}), bf16[64,75,4,128]{3,2,1,0:T(4,128)(2,1)}, u32[]{:S(2)}, u32[]{:S(2)}) %all-to-all-start.1) | async-done | bytes 4915232 | tf_op jit(solution)/shard_map/all_to_all | solution.py:150
  1066.2 7.4 copy.105
  (447 shorter events, 535.5 us)
Async XLA Ops:
  8.5 293.1 %all-to-all-start = ((bf16[1,75,256,128]{3,1,0,2:T(8,128)(2,1)}), bf16[1,75,256,128]{3,1,0,2:T(8,128)(2,1)}, u32[]{:S(2)}, u32[]{:S(2)}) async-start(bf16[1,75,256,128]{3,1,0,2:T(8,128)(2,1)} %copy.72), calls=%async_computation | async-start | bytes 10485760 | tf_op jit(solution)/shard_map/all_to_all | solution.py:109
  21.3 116.4 %collective-permute-start.2 = (bf16[75,1,128]{0,2,1:T(8,128)(2,1)S(1)}, bf16[75,1,128]{0,2,1:T(8,128)(2,1)S(1)}, u32[]{:S(2)}, u32[]{:S(2)}) collective-permute-start(bf16[75,1,128]{0,2,1:T(8,128)(2,1)S(1)} %get-tuple-element.133), channel_id=1, source_target_pairs={{4,0},{8,4},{12,8},{16,12},{20,16},{24,20},{28,24},{32,28},{36,32}... | collective-permute-start | bytes 57608 | tf_op jit(solution)/shard_map/ppermute | solution.py:28
  22.6 115.1 %collective-permute-start.1 = (bf16[75,1,128]{0,2,1:T(8,128)(2,1)S(1)}, bf16[75,1,128]{0,2,1:T(8,128)(2,1)S(1)}, u32[]{:S(2)}, u32[]{:S(2)}) collective-permute-start(bf16[75,1,128]{0,2,1:T(8,128)(2,1)S(1)} %get-tuple-element.132), channel_id=1, source_target_pairs={{0,4},{4,8},{8,12},{12,16},{16,20},{20,24},{24,28},{28,32},{32,36}... | collective-permute-start | bytes 57608 | tf_op jit(solution)/shard_map/ppermute | solution.py:27
  184.8 17.4 %collective-permute-start.16 = (f32[75,1,32]{0,2,1:T(8,128)S(1)}, f32[75,1,32]{0,2,1:T(8,128)S(1)}, u32[]{:S(2)}, u32[]{:S(2)}) collective-permute-start(f32[75,1,32]{0,2,1:T(8,128)S(1)} %multiply_bitcast_fusion.2), channel_id=1, source_target_pairs={{4,0},{8,4},{12,8},{16,12},{20,16},{24,20},{28,24},{32,28},{36,32}... | collective-permute-start | bytes 28808 | tf_op jit(solution)/shard_map/ppermute | solution.py:28
  186.1 16.1 %collective-permute-start.17 = (f32[75,1,32]{0,2,1:T(8,128)S(1)}, f32[75,1,32]{0,2,1:T(8,128)S(1)}, u32[]{:S(2)}, u32[]{:S(2)}) collective-permute-start(f32[75,1,32]{0,2,1:T(8,128)S(1)} %multiply_bitcast_fusion.2), channel_id=1, source_target_pairs={{0,4},{4,8},{8,12},{12,16},{16,20},{20,24},{24,28},{28,32},{32,36}... | collective-permute-start | bytes 28808 | tf_op jit(solution)/shard_map/ppermute | solution.py:27
  202.2 17.4 %collective-permute-start.20 = (f32[75,1,32]{0,2,1:T(8,128)S(1)}, f32[75,1,32]{0,2,1:T(8,128)S(1)}, u32[]{:S(2)}, u32[]{:S(2)}) collective-permute-start(f32[75,1,32]{0,2,1:T(8,128)S(1)} %fusion.369), channel_id=1, source_target_pairs={{4,0},{8,4},{12,8},{16,12},{20,16},{24,20},{28,24},{32,28},{36,32}... | collective-permute-start | bytes 28808 | tf_op jit(solution)/shard_map/ppermute | solution.py:28
  235.0 17.4 %collective-permute-start.30 = (bf16[75,1,64]{0,2,1:T(8,128)(2,1)S(1)}, bf16[75,1,64]{0,2,1:T(8,128)(2,1)S(1)}, u32[]{:S(2)}, u32[]{:S(2)}) collective-permute-start(bf16[75,1,64]{0,2,1:T(8,128)(2,1)S(1)} %get-tuple-element.173), channel_id=1, source_target_pairs={{4,0},{8,4},{12,8},{16,12},{20,16},{24,20},{28,24},{32,28},{36,32}... | collective-permute-start | bytes 28808 | tf_op jit(solution)/shard_map/ppermute | solution.py:28
  236.3 16.1 %collective-permute-start.29 = (bf16[75,1,64]{0,2,1:T(8,128)(2,1)S(1)}, bf16[75,1,64]{0,2,1:T(8,128)(2,1)S(1)}, u32[]{:S(2)}, u32[]{:S(2)}) collective-permute-start(bf16[75,1,64]{0,2,1:T(8,128)(2,1)S(1)} %get-tuple-element.172), channel_id=1, source_target_pairs={{0,4},{4,8},{8,12},{12,16},{16,20},{20,24},{24,28},{28,32},{32,36}... | collective-permute-start | bytes 28808 | tf_op jit(solution)/shard_map/ppermute | solution.py:27
  284.5 16.2 %collective-permute-start.43 = (bf16[75,4,1]{0,2,1:T(2,128)(2,1)S(1)}, bf16[75,4,1]{0,2,1:T(2,128)(2,1)S(1)}, u32[]{:S(2)}, u32[]{:S(2)}) collective-permute-start(bf16[75,4,1]{0,2,1:T(2,128)(2,1)S(1)} %get-tuple-element.123), channel_id=1, source_target_pairs={{1,0},{2,1},{3,2},{5,4},{6,5},{7,6},{9,8},{10,9},{11,10},{13,12},{... | collective-permute-start | bytes 1808 | tf_op jit(solution)/shard_map/ppermute | solution.py:28
  462.8 17.5 %collective-permute-start.60 = (f32[75,1,32]{0,2,1:T(8,128)S(1)}, f32[75,1,32]{0,2,1:T(8,128)S(1)}, u32[]{:S(2)}, u32[]{:S(2)}) collective-permute-start(f32[75,1,32]{0,2,1:T(8,128)S(1)} %multiply_bitcast_fusion.1), channel_id=1, source_target_pairs={{4,0},{8,4},{12,8},{16,12},{20,16},{24,20},{28,24},{32,28},{36,32}... | collective-permute-start | bytes 28808 | tf_op jit(solution)/shard_map/ppermute | solution.py:28
  464.1 16.3 %collective-permute-start.61 = (f32[75,1,32]{0,2,1:T(8,128)S(1)}, f32[75,1,32]{0,2,1:T(8,128)S(1)}, u32[]{:S(2)}, u32[]{:S(2)}) collective-permute-start(f32[75,1,32]{0,2,1:T(8,128)S(1)} %multiply_bitcast_fusion.1), channel_id=1, source_target_pairs={{0,4},{4,8},{8,12},{12,16},{16,20},{20,24},{24,28},{28,32},{32,36}... | collective-permute-start | bytes 28808 | tf_op jit(solution)/shard_map/ppermute | solution.py:27
  480.4 17.4 %collective-permute-start.64 = (f32[75,1,32]{0,2,1:T(8,128)S(1)}, f32[75,1,32]{0,2,1:T(8,128)S(1)}, u32[]{:S(2)}, u32[]{:S(2)}) collective-permute-start(f32[75,1,32]{0,2,1:T(8,128)S(1)} %fusion.341), channel_id=1, source_target_pairs={{4,0},{8,4},{12,8},{16,12},{20,16},{24,20},{28,24},{32,28},{36,32}... | collective-permute-start | bytes 28808 | tf_op jit(solution)/shard_map/ppermute | solution.py:28
  513.2 17.4 %collective-permute-start.74 = (bf16[75,1,64]{0,2,1:T(8,128)(2,1)S(1)}, bf16[75,1,64]{0,2,1:T(8,128)(2,1)S(1)}, u32[]{:S(2)}, u32[]{:S(2)}) collective-permute-start(bf16[75,1,64]{0,2,1:T(8,128)(2,1)S(1)} %get-tuple-element.157), channel_id=1, source_target_pairs={{4,0},{8,4},{12,8},{16,12},{20,16},{24,20},{28,24},{32,28},{36,32}... | collective-permute-start | bytes 28808 | tf_op jit(solution)/shard_map/ppermute | solution.py:28
  514.5 16.1 %collective-permute-start.73 = (bf16[75,1,64]{0,2,1:T(8,128)(2,1)S(1)}, bf16[75,1,64]{0,2,1:T(8,128)(2,1)S(1)}, u32[]{:S(2)}, u32[]{:S(2)}) collective-permute-start(bf16[75,1,64]{0,2,1:T(8,128)(2,1)S(1)} %get-tuple-element.156), channel_id=1, source_target_pairs={{0,4},{4,8},{8,12},{12,16},{16,20},{20,24},{24,28},{28,32},{32,36}... | collective-permute-start | bytes 28808 | tf_op jit(solution)/shard_map/ppermute | solution.py:27
  548.3 21.2 %collective-permute-start.83 = (bf16[75,4,1]{0,2,1:T(2,128)(2,1)}, bf16[75,4,1]{0,2,1:T(2,128)(2,1)S(1)}, u32[]{:S(2)}, u32[]{:S(2)}) collective-permute-start(bf16[75,4,1]{0,2,1:T(2,128)(2,1)} %get-tuple-element.111), channel_id=1, source_target_pairs={{1,0},{2,1},{3,2},{5,4},{6,5},{7,6},{9,8},{10,9},{11,10},{13,12},{... | collective-permute-start | bytes 1808 | tf_op jit(solution)/shard_map/ppermute | solution.py:28
  550.2 19.3 %collective-permute-start.80 = (bf16[75,4,1]{0,2,1:T(2,128)(2,1)}, bf16[75,4,1]{0,2,1:T(2,128)(2,1)}, u32[]{:S(2)}, u32[]{:S(2)}) collective-permute-start(bf16[75,4,1]{0,2,1:T(2,128)(2,1)} %get-tuple-element.110), channel_id=1, source_target_pairs={{0,1},{1,2},{2,3},{4,5},{5,6},{6,7},{8,9},{9,10},{10,11},{12,13},{... | collective-permute-start | bytes 1808 | tf_op jit(solution)/shard_map/ppermute | solution.py:27
  573.4 25.4 %collective-permute-start.87 = (bf16[75,4,1]{0,2,1:T(2,128)(2,1)}, bf16[75,4,1]{0,2,1:T(2,128)(2,1)S(1)}, u32[]{:S(2)}, u32[]{:S(2)}) collective-permute-start(bf16[75,4,1]{0,2,1:T(2,128)(2,1)} %get-tuple-element.107), channel_id=1, source_target_pairs={{1,0},{2,1},{3,2},{5,4},{6,5},{7,6},{9,8},{10,9},{11,10},{13,12},{... | collective-permute-start | bytes 1808 | tf_op jit(solution)/shard_map/ppermute | solution.py:28
  575.9 23.0 %collective-permute-start.84 = (bf16[75,4,1]{0,2,1:T(2,128)(2,1)}, bf16[75,4,1]{0,2,1:T(2,128)(2,1)}, u32[]{:S(2)}, u32[]{:S(2)}) collective-permute-start(bf16[75,4,1]{0,2,1:T(2,128)(2,1)} %get-tuple-element.106), channel_id=1, source_target_pairs={{0,1},{1,2},{2,3},{4,5},{5,6},{6,7},{8,9},{9,10},{10,11},{12,13},{... | collective-permute-start | bytes 1808 | tf_op jit(solution)/shard_map/ppermute | solution.py:27
  579.3 19.6 %collective-permute-start.86 = (bf16[75,1,128]{0,2,1:T(8,128)(2,1)}, bf16[75,1,128]{0,2,1:T(8,128)(2,1)S(1)}, u32[]{:S(2)}, u32[]{:S(2)}) collective-permute-start(bf16[75,1,128]{0,2,1:T(8,128)(2,1)} %get-tuple-element.105), channel_id=1, source_target_pairs={{4,0},{8,4},{12,8},{16,12},{20,16},{24,20},{28,24},{32,28},{36,32}... | collective-permute-start | bytes 57608 | tf_op jit(solution)/shard_map/ppermute | solution.py:28
  580.6 18.3 %collective-permute-start.85 = (bf16[75,1,128]{0,2,1:T(8,128)(2,1)}, bf16[75,1,128]{0,2,1:T(8,128)(2,1)}, u32[]{:S(2)}, u32[]{:S(2)}) collective-permute-start(bf16[75,1,128]{0,2,1:T(8,128)(2,1)} %get-tuple-element.104), channel_id=1, source_target_pairs={{0,4},{4,8},{8,12},{12,16},{16,20},{20,24},{24,28},{28,32},{32,36}... | collective-permute-start | bytes 57608 | tf_op jit(solution)/shard_map/ppermute | solution.py:27
  725.0 16.9 %collective-permute-start.104 = (f32[75,1,32]{0,2,1:T(8,128)S(1)}, f32[75,1,32]{0,2,1:T(8,128)S(1)}, u32[]{:S(2)}, u32[]{:S(2)}) collective-permute-start(f32[75,1,32]{0,2,1:T(8,128)S(1)} %multiply_bitcast_fusion), channel_id=1, source_target_pairs={{4,0},{8,4},{12,8},{16,12},{20,16},{24,20},{28,24},{32,28},{36,32}... | collective-permute-start | bytes 28808 | tf_op jit(solution)/shard_map/ppermute | solution.py:28
  741.9 17.4 %collective-permute-start.108 = (f32[75,1,32]{0,2,1:T(8,128)S(1)}, f32[75,1,32]{0,2,1:T(8,128)S(1)}, u32[]{:S(2)}, u32[]{:S(2)}) collective-permute-start(f32[75,1,32]{0,2,1:T(8,128)S(1)} %fusion.313), channel_id=1, source_target_pairs={{4,0},{8,4},{12,8},{16,12},{20,16},{24,20},{28,24},{32,28},{36,32}... | collective-permute-start | bytes 28808 | tf_op jit(solution)/shard_map/ppermute | solution.py:28
  774.8 17.5 %collective-permute-start.118 = (bf16[75,1,64]{0,2,1:T(8,128)(2,1)S(1)}, bf16[75,1,64]{0,2,1:T(8,128)(2,1)S(1)}, u32[]{:S(2)}, u32[]{:S(2)}) collective-permute-start(bf16[75,1,64]{0,2,1:T(8,128)(2,1)S(1)} %get-tuple-element.141), channel_id=1, source_target_pairs={{4,0},{8,4},{12,8},{16,12},{20,16},{24,20},{28,24},{32,28},{36,32}... | collective-permute-start | bytes 28808 | tf_op jit(solution)/shard_map/ppermute | solution.py:28
  776.1 16.2 %collective-permute-start.117 = (bf16[75,1,64]{0,2,1:T(8,128)(2,1)S(1)}, bf16[75,1,64]{0,2,1:T(8,128)(2,1)S(1)}, u32[]{:S(2)}, u32[]{:S(2)}) collective-permute-start(bf16[75,1,64]{0,2,1:T(8,128)(2,1)S(1)} %get-tuple-element.140), channel_id=1, source_target_pairs={{0,4},{4,8},{8,12},{12,16},{16,20},{20,24},{24,28},{28,32},{32,36}... | collective-permute-start | bytes 28808 | tf_op jit(solution)/shard_map/ppermute | solution.py:27
  792.4 16.3 %collective-permute-start.122 = (bf16[75,1,64]{0,2,1:T(8,128)(2,1)S(1)}, bf16[75,1,64]{0,2,1:T(8,128)(2,1)S(1)}, u32[]{:S(2)}, u32[]{:S(2)}) collective-permute-start(bf16[75,1,64]{0,2,1:T(8,128)(2,1)S(1)} %get-tuple-element.137), channel_id=1, source_target_pairs={{4,0},{8,4},{12,8},{16,12},{20,16},{24,20},{28,24},{32,28},{36,32}... | collective-permute-start | bytes 28808 | tf_op jit(solution)/shard_map/ppermute | solution.py:28
  810.8 21.1 %collective-permute-start.127 = (bf16[75,4,1]{0,2,1:T(2,128)(2,1)}, bf16[75,4,1]{0,2,1:T(2,128)(2,1)S(1)}, u32[]{:S(2)}, u32[]{:S(2)}) collective-permute-start(bf16[75,4,1]{0,2,1:T(2,128)(2,1)} %get-tuple-element.95), channel_id=1, source_target_pairs={{1,0},{2,1},{3,2},{5,4},{6,5},{7,6},{9,8},{10,9},{11,10},{13,12},{... | collective-permute-start | bytes 1808 | tf_op jit(solution)/shard_map/ppermute | solution.py:28
  812.7 19.2 %collective-permute-start.124 = (bf16[75,4,1]{0,2,1:T(2,128)(2,1)}, bf16[75,4,1]{0,2,1:T(2,128)(2,1)}, u32[]{:S(2)}, u32[]{:S(2)}) collective-permute-start(bf16[75,4,1]{0,2,1:T(2,128)(2,1)} %get-tuple-element.94), channel_id=1, source_target_pairs={{0,1},{1,2},{2,3},{4,5},{5,6},{6,7},{8,9},{9,10},{10,11},{12,13},{... | collective-permute-start | bytes 1808 | tf_op jit(solution)/shard_map/ppermute | solution.py:27
  835.8 25.4 %collective-permute-start.131 = (bf16[75,4,1]{0,2,1:T(2,128)(2,1)}, bf16[75,4,1]{0,2,1:T(2,128)(2,1)S(1)}, u32[]{:S(2)}, u32[]{:S(2)}) collective-permute-start(bf16[75,4,1]{0,2,1:T(2,128)(2,1)} %get-tuple-element.91), channel_id=1, source_target_pairs={{1,0},{2,1},{3,2},{5,4},{6,5},{7,6},{9,8},{10,9},{11,10},{13,12},{... | collective-permute-start | bytes 1808 | tf_op jit(solution)/shard_map/ppermute | solution.py:28
  838.3 23.0 %collective-permute-start.128 = (bf16[75,4,1]{0,2,1:T(2,128)(2,1)}, bf16[75,4,1]{0,2,1:T(2,128)(2,1)}, u32[]{:S(2)}, u32[]{:S(2)}) collective-permute-start(bf16[75,4,1]{0,2,1:T(2,128)(2,1)} %get-tuple-element.90), channel_id=1, source_target_pairs={{0,1},{1,2},{2,3},{4,5},{5,6},{6,7},{8,9},{9,10},{10,11},{12,13},{... | collective-permute-start | bytes 1808 | tf_op jit(solution)/shard_map/ppermute | solution.py:27
  841.7 19.6 %collective-permute-start.130 = (bf16[75,1,128]{0,2,1:T(8,128)(2,1)}, bf16[75,1,128]{0,2,1:T(8,128)(2,1)S(1)}, u32[]{:S(2)}, u32[]{:S(2)}) collective-permute-start(bf16[75,1,128]{0,2,1:T(8,128)(2,1)} %get-tuple-element.89), channel_id=1, source_target_pairs={{4,0},{8,4},{12,8},{16,12},{20,16},{24,20},{28,24},{32,28},{36,32}... | collective-permute-start | bytes 57608 | tf_op jit(solution)/shard_map/ppermute | solution.py:28
  843.0 18.3 %collective-permute-start.129 = (bf16[75,1,128]{0,2,1:T(8,128)(2,1)}, bf16[75,1,128]{0,2,1:T(8,128)(2,1)}, u32[]{:S(2)}, u32[]{:S(2)}) collective-permute-start(bf16[75,1,128]{0,2,1:T(8,128)(2,1)} %get-tuple-element.88), channel_id=1, source_target_pairs={{0,4},{4,8},{8,12},{12,16},{16,20},{20,24},{24,28},{28,32},{32,36}... | collective-permute-start | bytes 57608 | tf_op jit(solution)/shard_map/ppermute | solution.py:27
  948.7 117.5 %all-to-all-start.1 = ((bf16[64,75,4,128]{3,2,1,0:T(4,128)(2,1)}), bf16[64,75,4,128]{3,2,1,0:T(4,128)(2,1)}, u32[]{:S(2)}, u32[]{:S(2)}) async-start(bf16[64,75,4,128]{3,2,1,0:T(4,128)(2,1)} %reshape.181), calls=%async_computation.1 | async-start | bytes 9830400 | tf_op jit(solution)/shard_map/all_to_all | solution.py:150
  (115 other events, 1797.0 us)
where the time goes:
time: 1090 us; the launch traced here: 1070 us
  starting transfers between devices  471 us (43%)
  waiting for transfers between devices  274 us (25%)
  blocking collectives  178 us (16%)
  local copies, waits for them, and re-layouts  57.6 us (5%)
  other arithmetic  45 us (4%)
  matrix products  34.7 us (3%)
  between operations  13.1 us (1%)
    ppermute x66, starting transfers between devices, padded_2(): lax.ppermute(last, axis, up)  332 us
    psum x15, blocking collectives, by_axis(): x = lax.psum(x, axis)  178 us
    ppermute x66, waiting for transfers between devices, padded_2(): lax.ppermute(leading, axis, [(b, a) for a, b in up])  127 us
    ppermute x66, starting transfers between devices, padded_2(): lax.ppermute(leading, axis, [(b, a) for a, b in up])  121 us
    all_to_all x1, waiting for transfers between devices, local(): lax.all_to_all(final, ENS_GX, split_axis=0, concat_axis=2, tiled=True)  111 us
    ppermute x66, waiting for transfers between devices, padded_2(): lax.ppermute(last, axis, up)  35.8 us
    dot_general x4, matrix products, member_products(): jnp.einsum('ij,kjc->kic', spread, flat, preferred_element_type=jnp.float32)  34.7 us
    convert_element_type x4, other arithmetic, member_products(): product = (tiles * masked).astype(jnp.bfloat16)  22.4 us
  transfers between devices with their start and end apart: 134, of which 31 were waited for; matrix products, arithmetic and copies ran while one was open for 4% of the time, Pallas kernels for 0%

commit v1 on v0

v1 whole, which is shorter than its diff:
```python
import functools

import jax
import jax.numpy as jnp
from jax import lax
from jax.experimental import pallas as pl
from jax.experimental.pallas import tpu as pltpu
from jax.sharding import Mesh
from jax.sharding import PartitionSpec as P

ITERATIONS = 3
DIFFUSIVITY = 16.0
DAMPING = 0.8
ENS_GX = ("ens_0", "ens_1", "gx_0", "gx_1")
ALL = ENS_GX + ("gy",)
LAYERS = 75
PADDED = 76
TILE = 4
FLAT = PADDED * TILE
LANES = 128
STRIDE = 3
F32 = jnp.float32
BF16 = jnp.bfloat16


def swap_halves(first, second):
    upper = lax.broadcasted_iota(jnp.int32, first.shape, 1) < TILE
    return (
        jnp.where(upper, first, pltpu.roll(second, TILE, axis=1)),
        jnp.where(upper, pltpu.roll(first, TILE, axis=1), second),
    )


def to_blocks_kernel(members, out):
    half = PADDED // 2
    for group in range(2):
        rows = members[:, 16 * group : 16 * (group + 1), :].astype(F32)
        for part in range(2):
            chunk = rows[:, 8 * part : 8 * (part + 1), :]
            chunk = jnp.concatenate([chunk, jnp.zeros((1, 8, LANES), F32)], axis=0)
            pairs = chunk.reshape(half, 2, 8, LANES)
            low, high = swap_halves(pairs[:, 0], pairs[:, 1])
            block = 4 * group + 2 * part
            out[block] = low.reshape(FLAT, LANES).astype(BF16)
            out[block + 1] = high.reshape(FLAT, LANES).astype(BF16)


def to_blocks(members):
    layers, rows, lanes = members.shape
    return pl.pallas_call(
        to_blocks_kernel,
        grid=(rows // 32,),
        in_specs=[pl.BlockSpec((layers, 32, lanes), lambda s: (0, s, 0))],
        out_specs=pl.BlockSpec((8, FLAT, lanes), lambda s: (s, 0, 0)),
        out_shape=jax.ShapeDtypeStruct((rows // TILE, FLAT, lanes), BF16),
        name="to_blocks",
    )(members)


def ensemble_kernel(tiles, vector, mixing, out):
    step = pl.program_id(0)
    v = vector[...]
    total = jnp.zeros_like(v)
    for pair in range(tiles.shape[0] // 2):
        first = tiles[2 * pair].astype(F32)
        second = tiles[2 * pair + 1].astype(F32)
        u = jnp.concatenate([(first * v).astype(BF16), (second * v).astype(BF16)], axis=1)
        mixed = jnp.dot(mixing[...], u, preferred_element_type=F32)
        total = total + first * mixed[:, :LANES] + second * mixed[:, LANES:]

    @pl.when(step == 0)
    def _():
        out[...] = total

    @pl.when(step > 0)
    def _():
        out[...] = out[...] + total


def ensemble(tiles, vector, mixing):
    members = tiles.shape[0]
    return pl.pallas_call(
        ensemble_kernel,
        grid=(members // 8,),
        in_specs=[
            pl.BlockSpec((8, FLAT, LANES), lambda s: (s, 0, 0)),
            pl.BlockSpec((FLAT, LANES), lambda s: (0, 0)),
            pl.BlockSpec((FLAT, FLAT), lambda s: (0, 0)),
        ],
        out_specs=pl.BlockSpec((FLAT, LANES), lambda s: (0, 0)),
        out_shape=jax.ShapeDtypeStruct((FLAT, LANES), F32),
        cost_estimate=pl.CostEstimate(
            flops=2 * members * FLAT * FLAT * LANES,
            transcendentals=0,
            bytes_accessed=2 * members * FLAT * LANES,
        ),
        name="ensemble",
    )(tiles, vector, mixing)


def alpha_kernel(members, weights, mixing, out):
    half = PADDED // 2
    for group in range(2):
        parts = []
        for part in range(2):
            block = 4 * group + 2 * part
            u = [
                (
                    members[block + i].astype(F32)
                    * weights[0, (block + i) // 4, 0, (block + i) % 4].astype(F32)
                ).astype(BF16)
                for i in range(2)
            ]
            mixed = jnp.dot(mixing[...], jnp.concatenate(u, axis=1), preferred_element_type=F32)
            low = mixed[:, :LANES].reshape(half, 8, LANES)
            high = mixed[:, LANES:].reshape(half, 8, LANES)
            even, odd = swap_halves(low, high)
            parts.append(jnp.stack([even, odd], axis=1).reshape(PADDED, 8, LANES))
        rows = jnp.concatenate(parts, axis=1).astype(BF16)
        out[:, 16 * group : 16 * (group + 1), :] = rows[:LAYERS]


def alpha(members, weights, mixing):
    blocks = members.shape[0]
    return pl.pallas_call(
        alpha_kernel,
        grid=(blocks // 8,),
        in_specs=[
            pl.BlockSpec((8, FLAT, LANES), lambda s: (s, 0, 0)),
            pl.BlockSpec(
                (1, 2, 1, 4, FLAT, LANES), lambda s: ((s // 2) % 2, s % 2, s // 4, 0, 0, 0)
            ),
            pl.BlockSpec((FLAT, FLAT), lambda s: (0, 0)),
        ],
        out_specs=pl.BlockSpec((LAYERS, 32, LANES), lambda s: (0, s, 0)),
        out_shape=jax.ShapeDtypeStruct((LAYERS, TILE * blocks, LANES), BF16),
        name="alpha",
    )(members, weights, mixing)


def split_dot(left, right, exact_left):
    other = right if exact_left else left
    high = other.astype(BF16)
    low = (other - high.astype(F32)).astype(BF16)
    if exact_left:
        return jnp.dot(left, high, preferred_element_type=F32) + jnp.dot(
            left, low, preferred_element_type=F32
        )
    return jnp.dot(high, right, preferred_element_type=F32) + jnp.dot(
        low, right, preferred_element_type=F32
    )


def around(values):
    rows, columns = values.shape
    row = lax.broadcasted_iota(jnp.int32, values.shape, 0)
    column = lax.broadcasted_iota(jnp.int32, values.shape, 1)
    up = jnp.where(row == 0, 0.0, pltpu.roll(values, 1, axis=0))
    down = jnp.where(row == rows - 1, 0.0, pltpu.roll(values, rows - 1, axis=0))
    left = jnp.where(column == 0, 0.0, pltpu.roll(values, 1, axis=1))
    right = jnp.where(column == columns - 1, 0.0, pltpu.roll(values, columns - 1, axis=1))
    return (up + down) + (left + right)


def pairs_matrix(count, scale, transposed):
    shape = (count, 2 * count) if transposed else (2 * count, count)
    fine = lax.broadcasted_iota(jnp.int32, shape, 1 if transposed else 0)
    coarse = lax.broadcasted_iota(jnp.int32, shape, 0 if transposed else 1)
    return jnp.where(fine // 2 == coarse, scale, 0.0).astype(BF16)


def restrict(values):
    rows, columns = values.shape
    narrow = split_dot(values, pairs_matrix(columns // 2, 0.5, False), False)
    return split_dot(pairs_matrix(rows // 2, 0.5, True), narrow, True)


def prolong(values):
    rows, columns = values.shape
    tall = split_dot(pairs_matrix(rows, 1.0, False), values, True)
    return split_dot(tall, pairs_matrix(columns, 1.0, True), False)


def relax(values, source, strength):
    factor = DAMPING / (1.0 + 4.0 * strength)
    return (1.0 - DAMPING) * values + factor * (source + strength * around(values))


def cycle(source, level):
    strength = DIFFUSIVITY / 4.0**level
    factor = DAMPING / (1.0 + 4.0 * strength)
    values = factor * source
    if level == 2:
        for _ in range(3):
            values = relax(values, source, strength)
        return values
    values = relax(values, source, strength)
    remainder = source - ((1.0 + 4.0 * strength) * values - strength * around(values))
    values = values + prolong(cycle(restrict(remainder), level + 1))
    for _ in range(2):
        values = relax(values, source, strength)
    return values


def cycle_kernel(source, out):
    out[...] = cycle(source[...].astype(F32), 0)


def whole_cycle(source):
    return pl.pallas_call(
        cycle_kernel, out_shape=jax.ShapeDtypeStruct(source.shape, F32), name="cycle"
    )(source)


def flat(values):
    padded = jnp.pad(values, ((0, PADDED - LAYERS), (0, 0), (0, 0)))
    return padded.reshape(FLAT, LANES)


def thirds(value):
    first = lax.reduce_precision(value, 8, 7)
    second = lax.reduce_precision(value - first, 8, 7)
    return [first, second, value - first - second]


def local(members, spread, sea_mask, innovations, obs_error, static_scale):
    place = lax.axis_index(ALL)
    count = lax.axis_size(ALL)
    last = count - 1
    blocks = to_blocks(members.reshape(members.shape[1:]))

    mixing = (
        spread[:, None, :, None] * jnp.eye(TILE, dtype=spread.dtype)[None, :, None, :]
    ).reshape(LAYERS * TILE, LAYERS * TILE)
    mixing = jnp.pad(mixing, ((0, FLAT - LAYERS * TILE),) * 2)
    bound = 36.0 * jnp.max(jnp.sum(jnp.abs(spread.astype(F32)), axis=1)) + 67.0
    shrink = jnp.exp2(-jnp.ceil(jnp.log2(bound)))

    sea = jnp.broadcast_to(sea_mask.astype(F32)[None], (PADDED, TILE, LANES)).reshape(FLAT, LANES)
    scale = sea * flat(static_scale)
    error = shrink * flat(obs_error)
    outer = shrink * sea
    outer_scale = shrink * scale

    def exchange(vector, sums):
        source = (scale * vector).astype(BF16).reshape(PADDED, TILE, LANES)
        send = lax.pad(
            source,
            jnp.zeros((), BF16),
            ((0, count - (STRIDE * (PADDED - 1) + 1), STRIDE - 1), (0, 0, 0), (0, 0, 0)),
        )
        if sums is not None:
            parts = jnp.stack(thirds(sums[0]) + thirds(sums[1])).astype(BF16)
            row = jnp.pad(parts.reshape(1, 1, 6), ((0, 0), (0, TILE - 1), (0, LANES - 6)))
            slot = lax.broadcasted_iota(jnp.int32, (count, 1, 1), 0)
            send = jnp.where(slot == last, row, send)
        got = lax.all_to_all(send, ALL, split_axis=0, concat_axis=0, tiled=True)
        rows = count // 4
        grid = got.reshape(rows, 4, TILE, LANES).transpose(0, 2, 1, 3)
        solved = whole_cycle(grid.reshape(rows * TILE, 4 * LANES))
        back = solved.reshape(rows, TILE, 4, LANES).transpose(0, 2, 1, 3)
        back = back.reshape(count, TILE, LANES)
        if sums is not None:
            total = jnp.sum(got[:, 0, :8].astype(F32), axis=0)
            pair = jnp.stack([total[0] + total[1] + total[2], total[3] + total[4] + total[5]])
            pair = jnp.pad(pair.reshape(1, 1, 2), ((0, 0), (0, TILE - 1), (0, LANES - 2)))
            back = jnp.where(place == last, pair, back)
        result = lax.all_to_all(back, ALL, split_axis=0, concat_axis=0, tiled=True)
        term = result[: STRIDE * PADDED : STRIDE].reshape(FLAT, LANES)
        if sums is None:
            return term, None
        return term, (result[last, 0, 0], result[last, 0, 1])

    tiles = lax.all_to_all(blocks, ENS_GX, split_axis=0, concat_axis=0, tiled=True)

    def image_of(vector, sums):
        term, totals = exchange(vector, sums)
        spread_out = ensemble(tiles, sea * vector, mixing)
        return outer * spread_out + outer_scale * term + error * vector, totals

    def products(residual, along):
        return jnp.sum(residual * residual), jnp.sum(residual * along)

    residual = flat(innovations)
    image, _ = image_of(residual, None)
    weights = increment = direction = along = beyond = None
    norm_before = alpha_before = None
    for iteration in range(ITERATIONS):
        sums = products(residual, image)
        if iteration + 1 < ITERATIONS:
            image_next, (norm, product) = image_of(image, sums)
        else:
            mine = jnp.pad(jnp.stack(sums).reshape(1, 1, 2), ((0, 0), (0, 0), (0, LANES - 2)))
            got = lax.all_to_all(
                jnp.broadcast_to(mine, (count, 1, LANES)),
                ALL,
                split_axis=0,
                concat_axis=0,
                tiled=True,
            )
            norm, product = jnp.sum(got[:, 0, 0]), jnp.sum(got[:, 0, 1])
        if iteration == 0:
            alpha_now = norm / product
            direction, along = residual, image
            weights = alpha_now * direction
            increment = alpha_now * (along - error * direction)
        else:
            ratio = norm / norm_before
            alpha_now = norm / (product - ratio * norm / alpha_before)
            direction = residual + ratio * direction
            along = image + ratio * along
            weights = weights + alpha_now * direction
            increment = increment + alpha_now * (along - error * direction)
        if iteration + 1 < ITERATIONS:
            beyond = image_next if iteration == 0 else image_next + ratio * beyond
            residual = residual - alpha_now * along
            image = image - alpha_now * beyond
        norm_before, alpha_before = norm, alpha_now

    wide = (outer * weights).astype(BF16)[None]
    for axes in ("gx_1", "ens_0", ("ens_1", "gx_0")):
        wide = lax.all_gather(wide, axes, axis=0, tiled=True)
    fields = alpha(blocks, wide.reshape(2, 4, 2, 4, FLAT, LANES), mixing)
    increment = increment.reshape(PADDED, TILE, LANES)[:LAYERS]
    return increment, fields[None]


def solution(mesh):
    split = Mesh(mesh.devices.reshape(2, 2, 4, 4, mesh.shape["gy"]), ALL)
    return jax.shard_map(
        local,
        mesh=split,
        in_specs=(
            P(ENS_GX, None, None, "gy"),
            P(),
            P(ENS_GX, "gy"),
            P(None, ENS_GX, "gy"),
            P(None, ENS_GX, "gy"),
            P(None, ENS_GX, "gy"),
        ),
        out_specs=(P(None, ENS_GX, "gy"), P(ENS_GX, None, None, "gy")),
        check_vma=False,
    )
```

time: 1090 us -> 460 us (0.42); the launches traced: 1070 us -> 457 us
  starting transfers between devices: 471 us -> 32.9 us
  waiting for transfers between devices: 274 us -> 181 us
  blocking collectives: 178 us -> 92 us
  Pallas kernels: 0 us -> 56.8 us
  between operations: 13.1 us -> 51.9 us
  local copies, waits for them, and re-layouts: 57.6 us -> 22.4 us
  matrix products: 34.7 us -> 0 us
  other arithmetic: 45 us -> 19.9 us
    ppermute x132 -> x0, starting transfers between devices: 453 us -> none  [the longest x66 332 us: padded_2(): lax.ppermute(last, axis, up)]
    psum x15 -> x0, blocking collectives: 178 us -> none  [by_axis(): x = lax.psum(x, axis)]
    ppermute x132 -> x0, waiting for transfers between devices: 163 us -> none  [the longest x66 127 us: padded_2(): lax.ppermute(leading, axis, [(b, a) for a, b in up])]
    all_to_all x0 -> x3, blocking collectives: none -> 69.3 us  [the longest x2 50.7 us: exchange(): got = lax.all_to_all(send, ALL, split_axis=0, concat_axis=0, tiled=True)]
    pallas_call x0 -> x8, Pallas kernels: none -> 56.8 us  [the longest x3 23.5 us: ensemble(): pl.pallas_call(ensemble_kernel, grid=(members // 8,), in_specs=[pl.BlockS...]
    all_to_all x2 -> x5, waiting for transfers between devices: 111 us -> 148 us  [the longest x1 94.8 us: local(): lax.all_to_all(blocks, ENS_GX, split_axis=0, concat_axis=0, tiled=True)]
    dot_general x4 -> x0, matrix products: 34.7 us -> none  [member_products(): jnp.einsum('ij,kjc->kic', spread, flat, preferred_element_type=jnp.float32)]
    convert_element_type x53 -> x3, other arithmetic: 35.3 us -> 0.77 us  [the longest x1 0.68 us: local(): sea_mask.astype(F32)[None]]
  transfers between devices with their start and end apart: 134 -> 6, of which waited for: 31 -> 6; matrix products, arithmetic and copies ran while one was open for 4% -> 3% of each run, Pallas kernels for 0% -> 5%
where the time goes in v1:
time: 460 us; the launch traced here: 457 us
  waiting for transfers between devices  181 us (39%)
  blocking collectives  92 us (20%)
  Pallas kernels  56.8 us (12%)
  between operations  51.9 us (11%)
  starting transfers between devices  32.9 us (7%)
  local copies, waits for them, and re-layouts  22.4 us (5%)
  other arithmetic  19.9 us (4%)
    all_to_all x1, waiting for transfers between devices, local(): lax.all_to_all(blocks, ENS_GX, split_axis=0, concat_axis=0, tiled=True)  94.8 us
    all_to_all x2, blocking collectives, exchange(): got = lax.all_to_all(send, ALL, split_axis=0, concat_axis=0, tiled=True)  50.7 us
    all_to_all x3, waiting for transfers between devices, exchange(): result = lax.all_to_all(back, ALL, split_axis=0, concat_axis=0, tiled=True)  38.2 us
    all_gather x1, waiting for transfers between devices, local(): wide = lax.all_gather(wide, axes, axis=0, tiled=True)  32.7 us
    pallas_call x3, Pallas kernels, ensemble(): pl.pallas_call(ensemble_kernel, grid=(members // 8,), in_specs=[pl.BlockS...  23.5 us
    all_gather x2, blocking collectives, local(): wide = lax.all_gather(wide, axes, axis=0, tiled=True)  22.7 us
    all_to_all x3, starting transfers between devices, exchange(): result = lax.all_to_all(back, ALL, split_axis=0, concat_axis=0, tiled=True)  19.8 us
    all_to_all x1, blocking collectives, local(): lax.all_to_all(jnp.broadcast_to(mine, (count, 1, LANES)), ALL, split_axis...  18.6 us
  transfers between devices with their start and end apart: 6, of which 6 were waited for; matrix products, arithmetic and copies ran while one was open for 3% of the time, Pallas kernels for 5%

profile of v1, /device:TPU:8, one launch (start us, length us, event | category | flops | bytes accessed | tf_op | source)
XLA Modules:
  0.0 456.7 jit_solution(7228321558522653628)
XLA Ops:
  7.8 1.7 multiply_reduce_fusion.5
  10.7 29.4 %all_to_all.40 = bf16[256,4,128]{2,1,0:T(4,128)(2,1)S(1)} all-to-all(bf16[256,4,128]{2,1,0:T(4,128)(2,1)S(1)} %pad.44), channel_id=1, replica_groups=mesh['ens_0'=2,'ens_1'=2,'gx_0'=4,'gx_1'=4,'gy'=4] {'ens_0','ens_1','gx_..., dimensions={0} | all-to-all | bytes 524288 | tf_op jit(solution)/shard_map/all_to_all | solution.py:257
  41.0 5.4 %cycle.3 = f32[256,512]{1,0:T(8,128)} custom-call(bf16[256,512]{1,0:T(8,128)(2,1)} %bitcast.99), custom_call_target="tpu_custom_call" | custom-call | tf_op jit(solution)/shard_map/cycle/pallas_call | solution.py:210
  46.3 1.2 reshape.314
  48.5 6.5 %all-to-all-start.2 = ((f32[256,4,128]{2,1,0:T(4,128)}), f32[256,4,128]{2,1,0:T(4,128)S(1)}, u32[]{:S(2)}, u32[]{:S(2)}) async-start(f32[256,4,128]{2,1,0:T(4,128)} %bitcast.10), calls=%async_computation.2 | async-start | bytes 1048576 | tf_op jit(solution)/shard_map/all_to_all | solution.py:268
  55.0 7.6 %to_blocks.1.members = bf16[64,304,128]{2,1,0:T(8,128)(2,1)} custom-call(bf16[75,256,128]{2,1,0:T(8,128)(2,1)} %bitcast.87), custom_call_target="tpu_custom_call" | custom-call | tf_op jit(solution)/shard_map/to_blocks/pallas_call | solution.py:50
  62.6 12.9 %all-to-all-done.2 = f32[256,4,128]{2,1,0:T(4,128)S(1)} async-done(((f32[256,4,128]{2,1,0:T(4,128)}), f32[256,4,128]{2,1,0:T(4,128)S(1)}, u32[]{:S(2)}, u32[]{:S(2)}) %all-to-all-start.2) | async-done | bytes 524320 | tf_op jit(solution)/shard_map/all_to_all | solution.py:268
  75.5 5.7 %all-to-all-start = ((bf16[64,304,128]{2,1,0:T(8,128)(2,1)}), bf16[64,304,128]{2,1,0:T(8,128)(2,1)}, u32[]{:S(2)}, u32[]{:S(2)}) async-start(bf16[64,304,128]{2,1,0:T(8,128)(2,1)} %to_blocks.1.members), calls=%async_computation | async-start | bytes 9961472 | tf_op jit(solution)/shard_map/all_to_all | solution.py:274
  86.2 3.3 broadcast_multiply_fusion
  89.5 7.2 %mul.216 = bf16[300,300]{1,0:T(8,128)(2,1)S(1)} reshape(bf16[75,4,75,4]{3,2,1,0:T(8,128)(2,1)} %broadcast_multiply_fusion) | data formatting | bytes 360000 | tf_op jit(solution)/shard_map/mul | solution.py:233
  99.7 94.8 %all-to-all-done.tiles = bf16[64,304,128]{2,1,0:T(8,128)(2,1)} async-done(((bf16[64,304,128]{2,1,0:T(8,128)(2,1)}), bf16[64,304,128]{2,1,0:T(8,128)(2,1)}, u32[]{:S(2)}, u32[]{:S(2)}) %all-to-all-start) | async-done | bytes 4980768 | tf_op jit(solution)/shard_map/all_to_all | solution.py:274
  194.5 7.8 %ensemble.3 = f32[304,128]{1,0:T(8,128)} custom-call(bf16[64,304,128]{2,1,0:T(8,128)(2,1)} %all-to-all-done.tiles, f32[304,128]{1,0:T(8,128)} %mul.212.vector, bf16[304,304]{1,0:T(8,128)(2,1)} %pad.42.mixing), custom_call_target="tpu_custom_call" | custom-call | flops 1514143744 | bytes 4980736 | tf_op jit(solution)/shard_map/ensemble/pallas_call | solution.py:82
  202.3 1.7 fusion.11
  211.9 7.4 %all-to-all-start.3 = ((bf16[256,4,128]{2,1,0:T(4,128)(2,1)}), bf16[256,4,128]{2,1,0:T(4,128)(2,1)S(1)}, u32[]{:S(2)}, u32[]{:S(2)}) async-start(bf16[256,4,128]{2,1,0:T(4,128)(2,1)} %broadcast_select_fusion.1), calls=%async_computation.3 | async-start | bytes 524288 | tf_op jit(solution)/shard_map/all_to_all | solution.py:257
  219.3 15.0 %all-to-all-done.3 = bf16[256,4,128]{2,1,0:T(4,128)(2,1)S(1)} async-done(((bf16[256,4,128]{2,1,0:T(4,128)(2,1)}), bf16[256,4,128]{2,1,0:T(4,128)(2,1)S(1)}, u32[]{:S(2)}, u32[]{:S(2)}) %all-to-all-start.3) | async-done | bytes 262176 | tf_op jit(solution)/shard_map/all_to_all | solution.py:257
  239.9 5.4 %cycle.4 = f32[256,512]{1,0:T(8,128)} custom-call(bf16[256,512]{1,0:T(8,128)(2,1)} %bitcast.100), custom_call_target="tpu_custom_call" | custom-call | tf_op jit(solution)/shard_map/cycle/pallas_call | solution.py:210
  247.5 6.5 %all-to-all-start.4 = ((f32[256,4,128]{2,1,0:T(4,128)}), f32[256,4,128]{2,1,0:T(4,128)S(1)}, u32[]{:S(2)}, u32[]{:S(2)}) async-start(f32[256,4,128]{2,1,0:T(4,128)} %bitcast_select_fusion.1), calls=%async_computation.4 | async-start | bytes 1048576 | tf_op jit(solution)/shard_map/all_to_all | solution.py:268
  254.0 7.8 %ensemble.4 = f32[304,128]{1,0:T(8,128)} custom-call(bf16[64,304,128]{2,1,0:T(8,128)(2,1)} %all-to-all-done.tiles, f32[304,128]{1,0:T(8,128)} %get-tuple-element.16.vector, bf16[304,304]{1,0:T(8,128)(2,1)} %pad.42.mixing), custom_call_target="tpu_custom_call" | custom-call | flops 1514143744 | bytes 4980736 | tf_op jit(solution)/shard_map/ensemble/pallas_call | solution.py:82
  261.8 12.7 %all-to-all-done.4 = f32[256,4,128]{2,1,0:T(4,128)S(1)} async-done(((f32[256,4,128]{2,1,0:T(4,128)}), f32[256,4,128]{2,1,0:T(4,128)S(1)}, u32[]{:S(2)}, u32[]{:S(2)}) %all-to-all-start.4) | async-done | bytes 524320 | tf_op jit(solution)/shard_map/all_to_all | solution.py:268
  276.4 1.6 fusion.9
  290.4 21.3 %all_to_all.41 = bf16[256,4,128]{2,1,0:T(4,128)(2,1)S(1)} all-to-all(bf16[256,4,128]{2,1,0:T(4,128)(2,1)S(1)} %broadcast_select_fusion), channel_id=1, replica_groups=mesh['ens_0'=2,'ens_1'=2,'gx_0'=4,'gx_1'=4,'gy'=4] {'ens_0','ens_1','gx_..., dimensions={0} | all-to-all | bytes 524288 | tf_op jit(solution)/shard_map/all_to_all | solution.py:257
  317.3 5.4 %cycle.5 = f32[256,512]{1,0:T(8,128)} custom-call(bf16[256,512]{1,0:T(8,128)(2,1)} %bitcast.101), custom_call_target="tpu_custom_call" | custom-call | tf_op jit(solution)/shard_map/cycle/pallas_call | solution.py:210
  324.9 6.7 %all-to-all-start.6 = ((f32[256,4,128]{2,1,0:T(4,128)}), f32[256,4,128]{2,1,0:T(4,128)S(1)}, u32[]{:S(2)}, u32[]{:S(2)}) async-start(f32[256,4,128]{2,1,0:T(4,128)} %bitcast_select_fusion), calls=%async_computation.6 | async-start | bytes 1048576 | tf_op jit(solution)/shard_map/all_to_all | solution.py:268
  331.7 7.9 %ensemble.5 = f32[304,128]{1,0:T(8,128)} custom-call(bf16[64,304,128]{2,1,0:T(8,128)(2,1)} %all-to-all-done.tiles, f32[304,128]{1,0:T(8,128)} %get-tuple-element.13.vector, bf16[304,304]{1,0:T(8,128)(2,1)} %pad.42.mixing), custom_call_target="tpu_custom_call" | custom-call | flops 1514143744 | bytes 4980736 | tf_op jit(solution)/shard_map/ensemble/pallas_call | solution.py:82
  339.6 12.6 %all-to-all-done.6 = f32[256,4,128]{2,1,0:T(4,128)S(1)} async-done(((f32[256,4,128]{2,1,0:T(4,128)}), f32[256,4,128]{2,1,0:T(4,128)S(1)}, u32[]{:S(2)}, u32[]{:S(2)}) %all-to-all-start.6) | async-done | bytes 524320 | tf_op jit(solution)/shard_map/all_to_all | solution.py:268
  357.3 1.6 multiply_reduce_fusion.1
  358.9 1.4 maximum_bitcast_fusion.2
  360.4 18.6 %all_to_all.42 = f32[256,1,128]{2,1,0:T(1,128)S(1)} all-to-all(f32[256,1,128]{2,1,0:T(1,128)S(1)} %broadcast_in_dim.79), channel_id=1, replica_groups=mesh['ens_0'=2,'ens_1'=2,'gx_0'=4,'gx_1'=4,'gy'=4] {'ens_0','ens_1','gx_..., dimensions={0} | all-to-all | bytes 262144 | tf_op jit(solution)/shard_map/all_to_all | solution.py:294
  384.0 15.0 %all-gather = bf16[1216,128]{1,0:T(8,128)(2,1)S(1)} all-gather(bf16[304,128]{1,0:T(8,128)(2,1)S(1)} %get-tuple-element.8), channel_id=2, replica_groups=mesh['ens_0'=2,'ens_1'=2,'gx_0'=4,'gx_1'=4,'gy'=4] {'gx_1'}, dimensions={0}, use_global_device_ids=true | all-gather | bytes 389120 | tf_op jit(solution)/shard_map/all_gather | solution.py:322
  399.0 7.7 %all_gather.10 = bf16[8,304,128]{2,1,0:T(8,128)(2,1)} all-gather(bf16[4,304,128]{2,1,0:T(8,128)(2,1)S(1)} %bitcast.98), channel_id=1, replica_groups=mesh['ens_0'=2,'ens_1'=2,'gx_0'=4,'gx_1'=4,'gy'=4] {'ens_0'}, dimensions={0}, use_global_device_ids=true | all-gather | bytes 933888 | tf_op jit(solution)/shard_map/all_gather | solution.py:322
  407.5 32.7 %all-gather.3.cloned.1.call-done = bf16[64,304,128]{2,1,0:T(8,128)(2,1)} async-done(((bf16[8,304,128]{2,1,0:T(8,128)(2,1)}), bf16[64,304,128]{2,1,0:T(8,128)(2,1)}) %all-gather.3.cloned.1.call-update) | async-done | bytes 4980752 | tf_op jit(solution)/shard_map/all_gather | solution.py:322
  440.2 9.6 %alpha.1 = bf16[75,256,128]{2,1,0:T(8,128)(2,1)} custom-call(bf16[64,304,128]{2,1,0:T(8,128)(2,1)} %to_blocks.1.members, bf16[2,4,2,4,304,128]{5,4,3,2,1,0:T(8,128)(2,1)} %bitcast.86, bf16[304,304]{1,0:T(8,128)(2,1)} %pad.42.mixing), custom_call_target="tpu_custom_call" | custom-call | tf_op jit(solution)/shard_map/alpha/pallas_call | solution.py:125
  (59 shorter events, 22.7 us)
Async XLA Ops:
  48.5 27.1 %all-to-all-start.2 = ((f32[256,4,128]{2,1,0:T(4,128)}), f32[256,4,128]{2,1,0:T(4,128)S(1)}, u32[]{:S(2)}, u32[]{:S(2)}) async-start(f32[256,4,128]{2,1,0:T(4,128)} %bitcast.10), calls=%async_computation.2 | async-start | bytes 1048576 | tf_op jit(solution)/shard_map/all_to_all | solution.py:268
  62.6 23.5 %copy-start.1 = (bf16[75,75]{1,0:T(8,128)(2,1)S(1)}, bf16[75,75]{1,0:T(8,128)(2,1)}, u32[]{:S(2)}) copy-start(bf16[75,75]{1,0:T(8,128)(2,1)} %param.7) | copy-start | bytes 33754
  75.5 118.9 %all-to-all-start = ((bf16[64,304,128]{2,1,0:T(8,128)(2,1)}), bf16[64,304,128]{2,1,0:T(8,128)(2,1)}, u32[]{:S(2)}, u32[]{:S(2)}) async-start(bf16[64,304,128]{2,1,0:T(8,128)(2,1)} %to_blocks.1.members), calls=%async_computation | async-start | bytes 9961472 | tf_op jit(solution)/shard_map/all_to_all | solution.py:274
  89.5 10.1 %copy-start = (f32[75,4,128]{2,1,0:T(4,128)S(1)}, f32[75,4,128]{2,1,0:T(4,128)}, u32[]{:S(2)}) copy-start(f32[75,4,128]{2,1,0:T(4,128)} %param.10) | copy-start | bytes 460804
  211.9 22.4 %all-to-all-start.3 = ((bf16[256,4,128]{2,1,0:T(4,128)(2,1)}), bf16[256,4,128]{2,1,0:T(4,128)(2,1)S(1)}, u32[]{:S(2)}, u32[]{:S(2)}) async-start(bf16[256,4,128]{2,1,0:T(4,128)(2,1)} %broadcast_select_fusion.1), calls=%async_computation.3 | async-start | bytes 524288 | tf_op jit(solution)/shard_map/all_to_all | solution.py:257
  247.5 27.0 %all-to-all-start.4 = ((f32[256,4,128]{2,1,0:T(4,128)}), f32[256,4,128]{2,1,0:T(4,128)S(1)}, u32[]{:S(2)}, u32[]{:S(2)}) async-start(f32[256,4,128]{2,1,0:T(4,128)} %bitcast_select_fusion.1), calls=%async_computation.4 | async-start | bytes 1048576 | tf_op jit(solution)/shard_map/all_to_all | solution.py:268
  324.9 27.3 %all-to-all-start.6 = ((f32[256,4,128]{2,1,0:T(4,128)}), f32[256,4,128]{2,1,0:T(4,128)S(1)}, u32[]{:S(2)}, u32[]{:S(2)}) async-start(f32[256,4,128]{2,1,0:T(4,128)} %bitcast_select_fusion), calls=%async_computation.6 | async-start | bytes 1048576 | tf_op jit(solution)/shard_map/all_to_all | solution.py:268
  331.7 108.6 %all-gather.3.cloned.1.call-start = ((), (), s32[]{:S(2)}) async-start(), calls=%async_computation.8 | async-start | bytes 5603328 | tf_op jit(solution)/shard_map/all_gather | solution.py:322
Sparse Core Ops, SparseCore 0:
  406.8 33.3 all-gather.2

commit v2 on v1

--- a/solution.py
+++ b/solution.py
@@ -1,5 +1,3 @@
-import functools
-
 import jax
 import jax.numpy as jnp
 from jax import lax
@@ -8,7 +6,7 @@
 from jax.sharding import Mesh
 from jax.sharding import PartitionSpec as P
 
-ITERATIONS = 3
+
 DIFFUSIVITY = 16.0
 DAMPING = 0.8
 ENS_GX = ("ens_0", "ens_1", "gx_0", "gx_1")
@@ -202,14 +200,200 @@
     return values
 
 
-def cycle_kernel(source, out):
-    out[...] = cycle(source[...].astype(F32), 0)
-
-
-def whole_cycle(source):
+def cycle_kernel(place, got, out, grid):
+    count = got.shape[0]
+
+    @pl.when(place[0] < count - 2)
+    def _():
+        for slot in range(count):
+            rows, columns = TILE * (slot // 4), LANES * (slot % 4)
+            grid[rows : rows + TILE, columns : columns + LANES] = got[slot].astype(F32)
+        grid[...] = cycle(grid[...], 0)
+        for slot in range(count):
+            rows, columns = TILE * (slot // 4), LANES * (slot % 4)
+            out[slot] = grid[rows : rows + TILE, columns : columns + LANES]
+
+    @pl.when(place[0] >= count - 2)
+    def _():
+        lanes = jnp.sum(got[...].astype(F32), axis=0)
+        total = jnp.sum(jnp.sum(lanes, axis=0, keepdims=True), axis=1, keepdims=True)
+        out[...] = jnp.broadcast_to(total[None], out.shape)
+
+
+def whole_cycle(place, got):
+    count = got.shape[0]
     return pl.pallas_call(
-        cycle_kernel, out_shape=jax.ShapeDtypeStruct(source.shape, F32), name="cycle"
-    )(source)
+        cycle_kernel,
+        in_specs=[
+            pl.BlockSpec(memory_space=pltpu.SMEM),
+            pl.BlockSpec(memory_space=pltpu.VMEM),
+        ],
+        out_specs=pl.BlockSpec(memory_space=pltpu.VMEM),
+        out_shape=jax.ShapeDtypeStruct(got.shape, F32),
+        scratch_shapes=[pltpu.VMEM((count, 4 * LANES), F32)],
+        cost_estimate=pl.CostEstimate(
+            flops=400 * count * 4 * LANES, transcendentals=0, bytes_accessed=6 * got.size
+        ),
+        name="cycle",
+    )(place, got)
+
+
+def total_of(values):
+    return jnp.sum(jnp.sum(values, axis=0, keepdims=True), axis=1, keepdims=True)
+
+
+def unpack(result, term):
+    for layer in range(PADDED):
+        term[TILE * layer : TILE * (layer + 1), :] = result[STRIDE * layer]
+
+
+def pack(source, residual, image, send, term):
+    term[...] = source
+    send[...] = jnp.zeros(send.shape, BF16)
+    for layer in range(PADDED):
+        send[STRIDE * layer] = term[TILE * layer : TILE * (layer + 1), :].astype(BF16)
+    for slot, values in ((2, residual * residual), (1, residual * image)):
+        left = jnp.sum(values, axis=0, keepdims=True)
+        for part in range(3):
+            rounded = left.astype(BF16)
+            send[send.shape[0] - slot, part : part + 1, :] = rounded
+            left = left - rounded.astype(F32)
+
+
+def applied(result, spread_out, outer, outer_scale, error, vector, term):
+    unpack(result, term)
+    return outer[...] * spread_out[...] + outer_scale[...] * term[...] + error[...] * vector
+
+
+def totals(result):
+    count = result.shape[0]
+    return result[count - 2, 0:1, :], result[count - 1, 0:1, :]
+
+
+def start_kernel(
+    result, spread_out, scale, sea, outer, outer_scale, error, residual, image_out, masked, send, term
+):
+    r = residual[...]
+    w = applied(result, spread_out, outer, outer_scale, error, r, term)
+    image_out[...] = w
+    masked[...] = sea[...] * w
+    pack(scale[...] * w, r, w, send, term)
+
+
+def first_kernel(
+    result,
+    spread_out,
+    scale,
+    sea,
+    outer,
+    outer_scale,
+    error,
+    residual,
+    image,
+    residual_out,
+    image_out,
+    beyond_out,
+    masked,
+    send,
+    scalars,
+    term,
+):
+    r, w = residual[...], image[...]
+    z = applied(result, spread_out, outer, outer_scale, error, w, term)
+    norm, product = totals(result)
+    step = norm / product
+    beyond_out[...] = z
+    r_next = r - step * w
+    w_next = w - step * z
+    residual_out[...] = r_next
+    image_out[...] = w_next
+    masked[...] = sea[...] * w_next
+    scalars[0:1, :] = norm
+    scalars[1:2, :] = step
+    pack(scale[...] * w_next, r_next, w_next, send, term)
+
+
+def second_kernel(
+    result,
+    spread_out,
+    outer,
+    outer_scale,
+    error,
+    residual_0,
+    image_0,
+    beyond_0,
+    residual,
+    image,
+    scalars,
+    residual_out,
+    direction_out,
+    along_out,
+    weights_out,
+    increment_out,
+    image_out,
+    send,
+    scalars_out,
+    term,
+):
+    r, w = residual[...], image[...]
+    n = applied(result, spread_out, outer, outer_scale, error, w, term)
+    norm, product = totals(result)
+    norm_0, step_0 = scalars[0:1, :], scalars[1:2, :]
+    ratio = norm / norm_0
+    step = norm / (product - ratio * norm / step_0)
+    p = r + ratio * residual_0[...]
+    s = w + ratio * image_0[...]
+    z = n + ratio * beyond_0[...]
+    weights_out[...] = step_0 * residual_0[...] + step * p
+    increment_out[...] = step_0 * (image_0[...] - error[...] * residual_0[...]) + step * (
+        s - error[...] * p
+    )
+    r_next = r - step * s
+    w_next = w - step * z
+    residual_out[...] = r_next
+    direction_out[...] = p
+    along_out[...] = s
+    image_out[...] = w_next
+    scalars_out[0:1, :] = norm
+    scalars_out[1:2, :] = step
+    lane = lax.broadcasted_iota(jnp.int32, (1, LANES), 1)
+    both = jnp.where(lane < LANES // 2, total_of(r_next * r_next), total_of(r_next * w_next))
+    send[...] = jnp.broadcast_to(both[None], send.shape)
+
+
+def last_kernel(
+    got,
+    outer,
+    error,
+    residual,
+    direction,
+    along,
+    weights,
+    increment,
+    image,
+    scalars,
+    wide,
+    increment_out,
+):
+    both = jnp.sum(got[...], axis=0)
+    norm, product = both[:, 0:1], both[:, LANES // 2 : LANES // 2 + 1]
+    norm_1, step_1 = scalars[0:1, 0:1], scalars[1:2, 0:1]
+    ratio = norm / norm_1
+    step = norm / (product - ratio * norm / step_1)
+    p = residual[...] + ratio * direction[...]
+    s = image[...] + ratio * along[...]
+    wide[...] = (outer[...] * (weights[...] + step * p)).astype(BF16)
+    increment_out[...] = increment[...] + step * (s - error[...] * p)
+
+
+def kernel_call(body, arguments, outs, scratch=True):
+    return pl.pallas_call(
+        body,
+        in_specs=[pl.BlockSpec(memory_space=pltpu.VMEM)] * len(arguments),
+        out_specs=[pl.BlockSpec(memory_space=pltpu.VMEM)] * len(outs),
+        out_shape=[jax.ShapeDtypeStruct(shape, kind) for shape, kind in outs],
+        scratch_shapes=[pltpu.VMEM((FLAT, LANES), F32)] if scratch else [],
+    )(*arguments)
 
 
 def flat(values):
@@ -217,17 +401,28 @@
     return padded.reshape(FLAT, LANES)
 
 
-def thirds(value):
-    first = lax.reduce_precision(value, 8, 7)
-    second = lax.reduce_precision(value - first, 8, 7)
-    return [first, second, value - first - second]
-
-
-def local(members, spread, sea_mask, innovations, obs_error, static_scale):
-    place = lax.axis_index(ALL)
+def exchanged(values, axes):
+    return lax.all_to_all(values, axes, split_axis=0, concat_axis=0, tiled=True)
+
+
+def window(members, spread, sea_mask, innovations, obs_error, static_scale):
     count = lax.axis_size(ALL)
-    last = count - 1
+    place = lax.axis_index(ALL).astype(jnp.int32).reshape(1)
+    vector = ((FLAT, LANES), F32)
+    packed = ((count, TILE, LANES), BF16)
     blocks = to_blocks(members.reshape(members.shape[1:]))
+
+    sea = jnp.broadcast_to(sea_mask.astype(F32)[None], (PADDED, TILE, LANES)).reshape(FLAT, LANES)
+    scale = sea * flat(static_scale)
+    residual = flat(innovations)
+    source = (scale * residual).astype(BF16).reshape(PADDED, TILE, LANES)
+    send = lax.pad(
+        source,
+        jnp.zeros((), BF16),
+        ((0, count - (STRIDE * (PADDED - 1) + 1), STRIDE - 1), (0, 0, 0), (0, 0, 0)),
+    )
+    got = exchanged(send, ALL)
+    tiles = exchanged(blocks, ENS_GX)
 
     mixing = (
         spread[:, None, :, None] * jnp.eye(TILE, dtype=spread.dtype)[None, :, None, :]
@@ -235,89 +430,56 @@
     mixing = jnp.pad(mixing, ((0, FLAT - LAYERS * TILE),) * 2)
     bound = 36.0 * jnp.max(jnp.sum(jnp.abs(spread.astype(F32)), axis=1)) + 67.0
     shrink = jnp.exp2(-jnp.ceil(jnp.log2(bound)))
-
-    sea = jnp.broadcast_to(sea_mask.astype(F32)[None], (PADDED, TILE, LANES)).reshape(FLAT, LANES)
-    scale = sea * flat(static_scale)
     error = shrink * flat(obs_error)
     outer = shrink * sea
     outer_scale = shrink * scale
 
-    def exchange(vector, sums):
-        source = (scale * vector).astype(BF16).reshape(PADDED, TILE, LANES)
-        send = lax.pad(
-            source,
-            jnp.zeros((), BF16),
-            ((0, count - (STRIDE * (PADDED - 1) + 1), STRIDE - 1), (0, 0, 0), (0, 0, 0)),
-        )
-        if sums is not None:
-            parts = jnp.stack(thirds(sums[0]) + thirds(sums[1])).astype(BF16)
-            row = jnp.pad(parts.reshape(1, 1, 6), ((0, 0), (0, TILE - 1), (0, LANES - 6)))
-            slot = lax.broadcasted_iota(jnp.int32, (count, 1, 1), 0)
-            send = jnp.where(slot == last, row, send)
-        got = lax.all_to_all(send, ALL, split_axis=0, concat_axis=0, tiled=True)
-        rows = count // 4
-        grid = got.reshape(rows, 4, TILE, LANES).transpose(0, 2, 1, 3)
-        solved = whole_cycle(grid.reshape(rows * TILE, 4 * LANES))
-        back = solved.reshape(rows, TILE, 4, LANES).transpose(0, 2, 1, 3)
-        back = back.reshape(count, TILE, LANES)
-        if sums is not None:
-            total = jnp.sum(got[:, 0, :8].astype(F32), axis=0)
-            pair = jnp.stack([total[0] + total[1] + total[2], total[3] + total[4] + total[5]])
-            pair = jnp.pad(pair.reshape(1, 1, 2), ((0, 0), (0, TILE - 1), (0, LANES - 2)))
-            back = jnp.where(place == last, pair, back)
-        result = lax.all_to_all(back, ALL, split_axis=0, concat_axis=0, tiled=True)
-        term = result[: STRIDE * PADDED : STRIDE].reshape(FLAT, LANES)
-        if sums is None:
-            return term, None
-        return term, (result[last, 0, 0], result[last, 0, 1])
-
-    tiles = lax.all_to_all(blocks, ENS_GX, split_axis=0, concat_axis=0, tiled=True)
-
-    def image_of(vector, sums):
-        term, totals = exchange(vector, sums)
-        spread_out = ensemble(tiles, sea * vector, mixing)
-        return outer * spread_out + outer_scale * term + error * vector, totals
-
-    def products(residual, along):
-        return jnp.sum(residual * residual), jnp.sum(residual * along)
-
-    residual = flat(innovations)
-    image, _ = image_of(residual, None)
-    weights = increment = direction = along = beyond = None
-    norm_before = alpha_before = None
-    for iteration in range(ITERATIONS):
-        sums = products(residual, image)
-        if iteration + 1 < ITERATIONS:
-            image_next, (norm, product) = image_of(image, sums)
-        else:
-            mine = jnp.pad(jnp.stack(sums).reshape(1, 1, 2), ((0, 0), (0, 0), (0, LANES - 2)))
-            got = lax.all_to_all(
-                jnp.broadcast_to(mine, (count, 1, LANES)),
-                ALL,
-                split_axis=0,
-                concat_axis=0,
-                tiled=True,
-            )
-            norm, product = jnp.sum(got[:, 0, 0]), jnp.sum(got[:, 0, 1])
-        if iteration == 0:
-            alpha_now = norm / product
-            direction, along = residual, image
-            weights = alpha_now * direction
-            increment = alpha_now * (along - error * direction)
-        else:
-            ratio = norm / norm_before
-            alpha_now = norm / (product - ratio * norm / alpha_before)
-            direction = residual + ratio * direction
-            along = image + ratio * along
-            weights = weights + alpha_now * direction
-            increment = increment + alpha_now * (along - error * direction)
-        if iteration + 1 < ITERATIONS:
-            beyond = image_next if iteration == 0 else image_next + ratio * beyond
-            residual = residual - alpha_now * along
-            image = image - alpha_now * beyond
-        norm_before, alpha_before = norm, alpha_now
-
-    wide = (outer * weights).astype(BF16)[None]
+    def solve(received):
+        return exchanged(whole_cycle(place, received), ALL)
+
+    solved = whole_cycle(place, got)
+    result = exchanged(solved, ALL)
+    spread_out = ensemble(tiles, sea * residual, mixing)
+    constants = (outer, outer_scale, error)
+    image, masked, send = kernel_call(
+        start_kernel,
+        (result, spread_out, scale, sea) + constants + (residual,),
+        (vector, vector, packed),
+    )
+    result = solve(exchanged(send, ALL))
+    spread_out = ensemble(tiles, masked, mixing)
+    residual_1, image_1, beyond, masked, send, scalars = kernel_call(
+        first_kernel,
+        (result, spread_out, scale, sea) + constants + (residual, image),
+        (vector, vector, vector, vector, packed, ((8, LANES), F32)),
+    )
+    result = solve(exchanged(send, ALL))
+    spread_out = ensemble(tiles, masked, mixing)
+    residual_2, direction, along, weights, increment, image_2, send, scalars = kernel_call(
+        second_kernel,
+        (result, spread_out)
+        + constants
+        + (residual, image, beyond, residual_1, image_1, scalars),
+        (vector,) * 6 + (((count, 1, LANES), F32), ((8, LANES), F32)),
+    )
+    wide, increment = kernel_call(
+        last_kernel,
+        (
+            exchanged(send, ALL),
+            outer,
+            error,
+            residual_2,
+            direction,
+            along,
+            weights,
+            increment,
+            image_2,
+            scalars,
+        ),
+        (((FLAT, LANES), BF16), vector),
+        False,
+    )
+    wide = wide[None]
     for axes in ("gx_1", "ens_0", ("ens_1", "gx_0")):
         wide = lax.all_gather(wide, axes, axis=0, tiled=True)
     fields = alpha(blocks, wide.reshape(2, 4, 2, 4, FLAT, LANES), mixing)
@@ -328,7 +490,7 @@
 def solution(mesh):
     split = Mesh(mesh.devices.reshape(2, 2, 4, 4, mesh.shape["gy"]), ALL)
     return jax.shard_map(
-        local,
+        window,
         mesh=split,
         in_specs=(
             P(ENS_GX, None, None, "gy"),

time: 460 us -> 437 us (0.950)
  between operations: 51.9 us -> 14.9 us
  local copies, waits for them, and re-layouts: 22.4 us -> 35.2 us
  other arithmetic: 19.9 us -> 7.37 us
  Pallas kernels: 56.8 us -> 67.5 us
  waiting for transfers between devices: 181 us -> 173 us
  starting transfers between devices: 32.9 us -> 40.5 us
    pad x4 -> x2, local copies, waits for them, and re-layouts: 4.27 us -> 23.4 us  [the longest x1 22.6 us: window(): lax.pad(source, jnp.zeros((), BF16), ((0, count - (STRIDE * (PADDED - 1)...]
    pallas_call x3 -> x7, Pallas kernels: 16.1 us -> 26.7 us  [the longest x3 16.4 us: whole_cycle(): pl.pallas_call(cycle_kernel, in_specs=[pl.BlockSpec(memory_space=pltpu.SM...]
    all_to_all x5, starting transfers between devices: 32.8 us -> 40.5 us  [exchanged(): return lax.all_to_all(values, axes, split_axis=0, concat_axis=0, tiled=True)]
    all_to_all x5, waiting for transfers between devices: 148 us -> 140 us  [exchanged(): return lax.all_to_all(values, axes, split_axis=0, concat_axis=0, tiled=True)]
    reduce_sum x8 -> x1, other arithmetic: 6.34 us -> 0.1 us  [window(): bound = 36.0 * jnp.max(jnp.sum(jnp.abs(spread.astype(F32)), axis=1)) + 67.0]
  transfers between devices with their start and end apart: 6 -> 6, of which waited for: 6 -> 5; matrix products, arithmetic and copies ran while one was open for 3% -> 3% of each run, Pallas kernels for 5% -> 8%
where the time goes in v2:
time: 437 us; the launch traced here: 434 us
  waiting for transfers between devices  173 us (40%)
  blocking collectives  95.8 us (22%)
  Pallas kernels  67.5 us (15%)
  starting transfers between devices  40.5 us (9%)
  local copies, waits for them, and re-layouts  35.2 us (8%)
  between operations  14.9 us (3%)
  other arithmetic  7.37 us (2%)
    all_to_all x5, waiting for transfers between devices, exchanged(): return lax.all_to_all(values, axes, split_axis=0, concat_axis=0, tiled=True)  140 us
    all_to_all x3, blocking collectives, exchanged(): return lax.all_to_all(values, axes, split_axis=0, concat_axis=0, tiled=True)  72.4 us
    all_to_all x5, starting transfers between devices, exchanged(): return lax.all_to_all(values, axes, split_axis=0, concat_axis=0, tiled=True)  40.5 us
    all_gather x1, waiting for transfers between devices, window(): wide = lax.all_gather(wide, axes, axis=0, tiled=True)  32.5 us
    pallas_call x3, Pallas kernels, ensemble(): pl.pallas_call(ensemble_kernel, grid=(members // 8,), in_specs=[pl.BlockS...  23.5 us
    all_gather x2, blocking collectives, window(): wide = lax.all_gather(wide, axes, axis=0, tiled=True)  23.4 us
    pad x1, local copies, waits for them, and re-layouts, window(): lax.pad(source, jnp.zeros((), BF16), ((0, count - (STRIDE * (PADDED - 1)...  22.6 us
    pallas_call x3, Pallas kernels, whole_cycle(): pl.pallas_call(cycle_kernel, in_specs=[pl.BlockSpec(memory_space=pltpu.SM...  16.4 us
  transfers between devices with their start and end apart: 6, of which 5 were waited for; matrix products, arithmetic and copies ran while one was open for 3% of the time, Pallas kernels for 8%

profile of v2, /device:TPU:8, one launch (start us, length us, event | category | flops | bytes accessed | tf_op | source)
XLA Modules:
  0.0 434.3 jit_solution(3834556411822807204)
XLA Ops:
  7.8 1.1 fusion.1
  8.9 22.6 %pad.19 = bf16[256,4,128]{2,1,0:T(4,128)(2,1)} pad(bf16[76,4,128]{2,1,0:T(4,128)(2,1)S(1)} %get-tuple-element.45, bf16[]{:T(256)} %constant.40.clone.1), padding=0_30_2x0_0_0x0_0_0 | pad | bytes 339970 | tf_op jit(solution)/shard_map/pad | solution.py:419
  31.5 14.6 %all-to-all-start = ((bf16[256,4,128]{2,1,0:T(4,128)(2,1)}), bf16[256,4,128]{2,1,0:T(4,128)(2,1)S(1)}, u32[]{:S(2)}, u32[]{:S(2)}) async-start(bf16[256,4,128]{2,1,0:T(4,128)(2,1)} %pad.19), calls=%async_computation | async-start | bytes 524288 | tf_op jit(solution)/shard_map/all_to_all | solution.py:405
  46.2 7.6 %to_blocks.1.members = bf16[64,304,128]{2,1,0:T(8,128)(2,1)} custom-call(bf16[75,256,128]{2,1,0:T(8,128)(2,1)} %bitcast.11), custom_call_target="tpu_custom_call" | custom-call | tf_op jit(solution)/shard_map/to_blocks/pallas_call | solution.py:48
  53.8 7.4 %all-to-all-done.got = bf16[256,4,128]{2,1,0:T(4,128)(2,1)S(1)} async-done(((bf16[256,4,128]{2,1,0:T(4,128)(2,1)}), bf16[256,4,128]{2,1,0:T(4,128)(2,1)S(1)}, u32[]{:S(2)}, u32[]{:S(2)}) %all-to-all-start) | async-done | bytes 262176 | tf_op jit(solution)/shard_map/all_to_all | solution.py:405
  61.9 5.7 %all-to-all-start.2 = ((bf16[64,304,128]{2,1,0:T(8,128)(2,1)}), bf16[64,304,128]{2,1,0:T(8,128)(2,1)}, u32[]{:S(2)}, u32[]{:S(2)}) async-start(bf16[64,304,128]{2,1,0:T(8,128)(2,1)} %to_blocks.1.members), calls=%async_computation.2 | async-start | bytes 9961472 | tf_op jit(solution)/shard_map/all_to_all | solution.py:405
  67.6 5.5 %cycle.3 = f32[256,4,128]{2,1,0:T(4,128)} custom-call(s32[1]{0:T(128)} %bitcast.place, bf16[256,4,128]{2,1,0:T(4,128)(2,1)} %copy-done.5), custom_call_target="tpu_custom_call" | custom-call | flops 52428800 | bytes 786432 | tf_op jit(solution)/shard_map/cycle/pallas_call | solution.py:225
  73.0 107.8 %all-to-all-done.2.tiles = bf16[64,304,128]{2,1,0:T(8,128)(2,1)} async-done(((bf16[64,304,128]{2,1,0:T(8,128)(2,1)}), bf16[64,304,128]{2,1,0:T(8,128)(2,1)}, u32[]{:S(2)}, u32[]{:S(2)}) %all-to-all-start.2) | async-done | bytes 4980768 | tf_op jit(solution)/shard_map/all_to_all | solution.py:405
  180.8 7.2 %all-to-all-start.1 = ((f32[256,4,128]{2,1,0:T(4,128)}), f32[256,4,128]{2,1,0:T(4,128)S(1)}, u32[]{:S(2)}, u32[]{:S(2)}) async-start(f32[256,4,128]{2,1,0:T(4,128)} %cycle.3), calls=%async_computation.1 | async-start | bytes 1048576 | tf_op jit(solution)/shard_map/all_to_all | solution.py:405
  189.5 3.3 broadcast_multiply_fusion
  192.8 7.1 %mul.69 = bf16[300,300]{1,0:T(8,128)(2,1)S(1)} reshape(bf16[75,4,75,4]{3,2,1,0:T(8,128)(2,1)} %broadcast_multiply_fusion) | data formatting | bytes 360000 | tf_op jit(solution)/shard_map/mul | solution.py:428
  202.3 7.8 %ensemble.3.spread_out = f32[304,128]{1,0:T(8,128)} custom-call(bf16[64,304,128]{2,1,0:T(8,128)(2,1)} %all-to-all-done.2.tiles, f32[304,128]{1,0:T(8,128)} %get-tuple-element.43.vector, bf16[304,304]{1,0:T(8,128)(2,1)} %pad.20.mixing), custom_call_target="tpu_custom_call" | custom-call | flops 1514143744 | bytes 4980736 | tf_op jit(solution)/shard_map/ensemble/pallas_call | solution.py:80
  211.0 2.4 shard_map.77
  213.4 28.8 %all_to_all.40.got = bf16[256,4,128]{2,1,0:T(4,128)(2,1)} all-to-all(bf16[256,4,128]{2,1,0:T(4,128)(2,1)} %get-tuple-element.21), channel_id=1, replica_groups=mesh['ens_0'=2,'ens_1'=2,'gx_0'=4,'gx_1'=4,'gy'=4] {'ens_0','ens_1','gx_..., dimensions={0} | all-to-all | bytes 524288 | tf_op jit(solution)/shard_map/all_to_all | solution.py:405
  242.2 5.5 %cycle.4 = f32[256,4,128]{2,1,0:T(4,128)} custom-call(s32[1]{0:T(128)} %bitcast.place, bf16[256,4,128]{2,1,0:T(4,128)(2,1)} %all_to_all.40.got), custom_call_target="tpu_custom_call" | custom-call | flops 52428800 | bytes 786432 | tf_op jit(solution)/shard_map/cycle/pallas_call | solution.py:225
  247.7 6.5 %all-to-all-start.4 = ((f32[256,4,128]{2,1,0:T(4,128)}), f32[256,4,128]{2,1,0:T(4,128)S(1)}, u32[]{:S(2)}, u32[]{:S(2)}) async-start(f32[256,4,128]{2,1,0:T(4,128)} %cycle.4), calls=%async_computation.4 | async-start | bytes 1048576 | tf_op jit(solution)/shard_map/all_to_all | solution.py:405
  254.2 7.8 %ensemble.4.spread_out = f32[304,128]{1,0:T(8,128)} custom-call(bf16[64,304,128]{2,1,0:T(8,128)(2,1)} %all-to-all-done.2.tiles, f32[304,128]{1,0:T(8,128)} %get-tuple-element.22.vector, bf16[304,304]{1,0:T(8,128)(2,1)} %pad.20.mixing), custom_call_target="tpu_custom_call" | custom-call | flops 1514143744 | bytes 4980736 | tf_op jit(solution)/shard_map/ensemble/pallas_call | solution.py:80
  262.0 12.7 %all-to-all-done.4.result = f32[256,4,128]{2,1,0:T(4,128)S(1)} async-done(((f32[256,4,128]{2,1,0:T(4,128)}), f32[256,4,128]{2,1,0:T(4,128)S(1)}, u32[]{:S(2)}, u32[]{:S(2)}) %all-to-all-start.4) | async-done | bytes 524320 | tf_op jit(solution)/shard_map/all_to_all | solution.py:405
  275.5 2.7 shard_map.78
  278.2 22.8 %all_to_all.41.got = bf16[256,4,128]{2,1,0:T(4,128)(2,1)} all-to-all(bf16[256,4,128]{2,1,0:T(4,128)(2,1)} %get-tuple-element.24), channel_id=1, replica_groups=mesh['ens_0'=2,'ens_1'=2,'gx_0'=4,'gx_1'=4,'gy'=4] {'ens_0','ens_1','gx_..., dimensions={0} | all-to-all | bytes 524288 | tf_op jit(solution)/shard_map/all_to_all | solution.py:405
  300.9 5.5 %cycle.5 = f32[256,4,128]{2,1,0:T(4,128)} custom-call(s32[1]{0:T(128)} %bitcast.place, bf16[256,4,128]{2,1,0:T(4,128)(2,1)} %all_to_all.41.got), custom_call_target="tpu_custom_call" | custom-call | flops 52428800 | bytes 786432 | tf_op jit(solution)/shard_map/cycle/pallas_call | solution.py:225
  306.4 6.5 %all-to-all-start.6 = ((f32[256,4,128]{2,1,0:T(4,128)}), f32[256,4,128]{2,1,0:T(4,128)S(1)}, u32[]{:S(2)}, u32[]{:S(2)}) async-start(f32[256,4,128]{2,1,0:T(4,128)} %cycle.5), calls=%async_computation.6 | async-start | bytes 1048576 | tf_op jit(solution)/shard_map/all_to_all | solution.py:405
  313.0 7.8 %ensemble.5.spread_out = f32[304,128]{1,0:T(8,128)} custom-call(bf16[64,304,128]{2,1,0:T(8,128)(2,1)} %all-to-all-done.2.tiles, f32[304,128]{1,0:T(8,128)} %get-tuple-element.25.vector, bf16[304,304]{1,0:T(8,128)(2,1)} %pad.20.mixing), custom_call_target="tpu_custom_call" | custom-call | flops 1514143744 | bytes 4980736 | tf_op jit(solution)/shard_map/ensemble/pallas_call | solution.py:80
  320.8 12.6 %all-to-all-done.6.result = f32[256,4,128]{2,1,0:T(4,128)S(1)} async-done(((f32[256,4,128]{2,1,0:T(4,128)}), f32[256,4,128]{2,1,0:T(4,128)S(1)}, u32[]{:S(2)}, u32[]{:S(2)}) %all-to-all-start.6) | async-done | bytes 524320 | tf_op jit(solution)/shard_map/all_to_all | solution.py:405
  334.3 2.7 shard_map.79
  336.9 20.8 %all_to_all.42.got = f32[256,1,128]{2,1,0:T(1,128)} all-to-all(f32[256,1,128]{2,1,0:T(1,128)} %get-tuple-element.30), channel_id=1, replica_groups=mesh['ens_0'=2,'ens_1'=2,'gx_0'=4,'gx_1'=4,'gy'=4] {'ens_0','ens_1','gx_..., dimensions={0} | all-to-all | bytes 262144 | tf_op jit(solution)/shard_map/all_to_all | solution.py:405
  357.7 2.6 shard_map.80
  360.2 15.8 %all-gather = bf16[1216,128]{1,0:T(8,128)(2,1)S(1)} all-gather(bf16[304,128]{1,0:T(8,128)(2,1)} %get-tuple-element.39), channel_id=2, replica_groups=mesh['ens_0'=2,'ens_1'=2,'gx_0'=4,'gx_1'=4,'gy'=4] {'gx_1'}, dimensions={0}, use_global_device_ids=true | all-gather | bytes 389120 | tf_op jit(solution)/shard_map/all_gather | solution.py:484
  376.0 7.7 %all_gather.10 = bf16[8,304,128]{2,1,0:T(8,128)(2,1)} all-gather(bf16[4,304,128]{2,1,0:T(8,128)(2,1)S(1)} %bitcast.24), channel_id=1, replica_groups=mesh['ens_0'=2,'ens_1'=2,'gx_0'=4,'gx_1'=4,'gy'=4] {'ens_0'}, dimensions={0}, use_global_device_ids=true | all-gather | bytes 933888 | tf_op jit(solution)/shard_map/all_gather | solution.py:484
  383.7 1.6 slice.7
  385.3 32.5 %all-gather.3.cloned.1.call-done = bf16[64,304,128]{2,1,0:T(8,128)(2,1)} async-done(((bf16[8,304,128]{2,1,0:T(8,128)(2,1)}), bf16[64,304,128]{2,1,0:T(8,128)(2,1)}) %all-gather.3.cloned.1.call-update) | async-done | bytes 4980752 | tf_op jit(solution)/shard_map/all_gather | solution.py:484
  417.9 9.6 %alpha.1 = bf16[75,256,128]{2,1,0:T(8,128)(2,1)} custom-call(bf16[64,304,128]{2,1,0:T(8,128)(2,1)} %to_blocks.1.members, bf16[2,4,2,4,304,128]{5,4,3,2,1,0:T(8,128)(2,1)} %bitcast.10, bf16[304,304]{1,0:T(8,128)(2,1)} %pad.20.mixing), custom_call_target="tpu_custom_call" | custom-call | tf_op jit(solution)/shard_map/alpha/pallas_call | solution.py:123
  (27 shorter events, 6.9 us)
Async XLA Ops:
  8.9 192.5 %copy-start = (f32[76,4,128]{2,1,0:T(4,128)}, f32[76,4,128]{2,1,0:T(4,128)S(1)}, u32[]{:S(2)}) copy-start(f32[76,4,128]{2,1,0:T(4,128)S(1)} %get-tuple-element.46) | copy-start | bytes 466948
  31.5 29.6 %all-to-all-start = ((bf16[256,4,128]{2,1,0:T(4,128)(2,1)}), bf16[256,4,128]{2,1,0:T(4,128)(2,1)S(1)}, u32[]{:S(2)}, u32[]{:S(2)}) async-start(bf16[256,4,128]{2,1,0:T(4,128)(2,1)} %pad.19), calls=%async_computation | async-start | bytes 524288 | tf_op jit(solution)/shard_map/all_to_all | solution.py:405
  53.8 134.2 %copy-start.7 = (bf16[75,75]{1,0:T(8,128)(2,1)S(1)}, bf16[75,75]{1,0:T(8,128)(2,1)}, u32[]{:S(2)}) copy-start(bf16[75,75]{1,0:T(8,128)(2,1)} %param.7) | copy-start | bytes 33754
  61.2 0.7 copy-start.5
  61.9 118.9 %all-to-all-start.2 = ((bf16[64,304,128]{2,1,0:T(8,128)(2,1)}), bf16[64,304,128]{2,1,0:T(8,128)(2,1)}, u32[]{:S(2)}, u32[]{:S(2)}) async-start(bf16[64,304,128]{2,1,0:T(8,128)(2,1)} %to_blocks.1.members), calls=%async_computation.2 | async-start | bytes 9961472 | tf_op jit(solution)/shard_map/all_to_all | solution.py:405
  180.8 29.4 %all-to-all-start.1 = ((f32[256,4,128]{2,1,0:T(4,128)}), f32[256,4,128]{2,1,0:T(4,128)S(1)}, u32[]{:S(2)}, u32[]{:S(2)}) async-start(f32[256,4,128]{2,1,0:T(4,128)} %cycle.3), calls=%async_computation.1 | async-start | bytes 1048576 | tf_op jit(solution)/shard_map/all_to_all | solution.py:405
  189.5 11.2 %copy-start.6 = (f32[75,4,128]{2,1,0:T(4,128)S(1)}, f32[75,4,128]{2,1,0:T(4,128)}, u32[]{:S(2)}) copy-start(f32[75,4,128]{2,1,0:T(4,128)} %param.10) | copy-start | bytes 460804
  201.4 8.7 %copy-start.1 = (f32[76,4,128]{2,1,0:T(4,128)}, f32[76,4,128]{2,1,0:T(4,128)S(1)}, u32[]{:S(2)}) copy-start(f32[76,4,128]{2,1,0:T(4,128)S(1)} %broadcast_in_dim.6) | copy-start | bytes 466948
  210.2 0.8 copy-start.2
  247.7 27.0 %all-to-all-start.4 = ((f32[256,4,128]{2,1,0:T(4,128)}), f32[256,4,128]{2,1,0:T(4,128)S(1)}, u32[]{:S(2)}, u32[]{:S(2)}) async-start(f32[256,4,128]{2,1,0:T(4,128)} %cycle.4), calls=%async_computation.4 | async-start | bytes 1048576 | tf_op jit(solution)/shard_map/all_to_all | solution.py:405
  274.7 0.8 copy-start.3
  306.4 27.0 %all-to-all-start.6 = ((f32[256,4,128]{2,1,0:T(4,128)}), f32[256,4,128]{2,1,0:T(4,128)S(1)}, u32[]{:S(2)}, u32[]{:S(2)}) async-start(f32[256,4,128]{2,1,0:T(4,128)} %cycle.5), calls=%async_computation.6 | async-start | bytes 1048576 | tf_op jit(solution)/shard_map/all_to_all | solution.py:405
  312.9 104.9 %all-gather.3.cloned.1.call-start = ((), (), s32[]{:S(2)}) async-start(), calls=%async_computation.8 | async-start | bytes 5603328 | tf_op jit(solution)/shard_map/all_gather | solution.py:484
  333.5 0.8 copy-start.4
Sparse Core Ops, SparseCore 0:
  383.8 33.9 all-gather.2

commit v3 on v2

--- a/solution.py
+++ b/solution.py
@@ -96,16 +96,24 @@
     )(tiles, vector, mixing)
 
 
-def alpha_kernel(members, weights, mixing, out):
+def alpha_kernel(members, first, pair, coefficients, mixing, out):
     half = PADDED // 2
+    factors = [coefficients[i : i + 1, :] for i in range(3)]
+
+    def weights(x, z):
+        return (
+            factors[0] * first[0, x, z, 0].astype(F32)
+            + factors[1] * pair[0, x, z, 0, 0].astype(F32)
+            + factors[2] * pair[0, x, z, 0, 1].astype(F32)
+        )
+
     for group in range(2):
         parts = []
         for part in range(2):
             block = 4 * group + 2 * part
             u = [
                 (
-                    members[block + i].astype(F32)
-                    * weights[0, (block + i) // 4, 0, (block + i) % 4].astype(F32)
+                    members[block + i].astype(F32) * weights((block + i) // 4, (block + i) % 4)
                 ).astype(BF16)
                 for i in range(2)
             ]
@@ -118,7 +126,7 @@
         out[:, 16 * group : 16 * (group + 1), :] = rows[:LAYERS]
 
 
-def alpha(members, weights, mixing):
+def alpha(members, first, pair, coefficients, mixing):
     blocks = members.shape[0]
     return pl.pallas_call(
         alpha_kernel,
@@ -126,14 +134,18 @@
         in_specs=[
             pl.BlockSpec((8, FLAT, LANES), lambda s: (s, 0, 0)),
             pl.BlockSpec(
-                (1, 2, 1, 4, FLAT, LANES), lambda s: ((s // 2) % 2, s % 2, s // 4, 0, 0, 0)
+                (1, 2, 4, 1, FLAT, LANES), lambda s: ((s // 2) % 2, s % 2, 0, s // 4, 0, 0)
             ),
+            pl.BlockSpec(
+                (1, 2, 4, 1, 2, FLAT, LANES), lambda s: ((s // 2) % 2, s % 2, 0, s // 4, 0, 0, 0)
+            ),
+            pl.BlockSpec((8, LANES), lambda s: (0, 0)),
             pl.BlockSpec((FLAT, FLAT), lambda s: (0, 0)),
         ],
         out_specs=pl.BlockSpec((LAYERS, 32, LANES), lambda s: (0, s, 0)),
         out_shape=jax.ShapeDtypeStruct((LAYERS, TILE * blocks, LANES), BF16),
         name="alpha",
-    )(members, weights, mixing)
+    )(members, first, pair, coefficients, mixing)
 
 
 def split_dot(left, right, exact_left):
@@ -260,6 +272,59 @@
             left = left - rounded.astype(F32)
 
 
+def prepare_kernel(
+    innovations, static_scale, sea_mask, residual, scale, sea, masked, halves, send, term
+):
+    mask = sea_mask[...].astype(F32)
+    for layer in range(PADDED):
+        rows = slice(TILE * layer, TILE * (layer + 1))
+        if layer < LAYERS:
+            residual[rows, :] = innovations[layer]
+            scale[rows, :] = mask * static_scale[layer]
+        else:
+            residual[rows, :] = jnp.zeros((TILE, LANES), F32)
+            scale[rows, :] = jnp.zeros((TILE, LANES), F32)
+        sea[rows, :] = mask
+    r = residual[...]
+    first = sea[...] * r
+    masked[...] = first
+    high = first.astype(BF16)
+    halves[0] = high
+    halves[1] = (first - high.astype(F32)).astype(BF16)
+    term[...] = scale[...] * r
+    send[...] = jnp.zeros(send.shape, BF16)
+    for layer in range(PADDED):
+        send[STRIDE * layer] = term[TILE * layer : TILE * (layer + 1), :].astype(BF16)
+
+
+def constants_kernel(spread, obs_error, scale, sea, mixing, error, outer, outer_scale, shrinks):
+    values = spread[...]
+    sums = jnp.sum(jnp.abs(values.astype(F32)), axis=1, keepdims=True)
+    bound = 36.0 * jnp.max(sums, axis=0, keepdims=True) + 67.0
+    shrink = jnp.exp2(-jnp.ceil(jnp.log2(jnp.broadcast_to(bound, (8, LANES)))))
+    shrinks[...] = shrink
+    row = shrink[0:1, :]
+    for layer in range(PADDED):
+        rows = slice(TILE * layer, TILE * (layer + 1))
+        if layer < LAYERS:
+            error[rows, :] = row * obs_error[layer]
+        else:
+            error[rows, :] = jnp.zeros((TILE, LANES), F32)
+    outer[...] = row * sea[...]
+    outer_scale[...] = row * scale[...]
+
+    def chooser(shape, long):
+        place = lax.broadcasted_iota(jnp.int32, shape, long)
+        layer = lax.broadcasted_iota(jnp.int32, shape, 1 - long)
+        return jnp.where(place // TILE == layer, 1.0, 0.0).astype(BF16)
+
+    tall = jnp.dot(chooser((FLAT, LAYERS), 0), values, preferred_element_type=F32).astype(BF16)
+    full = jnp.dot(tall, chooser((LAYERS, FLAT), 1), preferred_element_type=F32)
+    row_in = lax.broadcasted_iota(jnp.int32, full.shape, 0) % TILE
+    column_in = lax.broadcasted_iota(jnp.int32, full.shape, 1) % TILE
+    mixing[...] = jnp.where(row_in == column_in, full, 0.0).astype(BF16)
+
+
 def applied(result, spread_out, outer, outer_scale, error, vector, term):
     unpack(result, term)
     return outer[...] * spread_out[...] + outer_scale[...] * term[...] + error[...] * vector
@@ -271,7 +336,18 @@
 
 
 def start_kernel(
-    result, spread_out, scale, sea, outer, outer_scale, error, residual, image_out, masked, send, term
+    result,
+    spread_out,
+    scale,
+    sea,
+    outer,
+    outer_scale,
+    error,
+    residual,
+    image_out,
+    masked,
+    send,
+    term,
 ):
     r = residual[...]
     w = applied(result, spread_out, outer, outer_scale, error, r, term)
@@ -294,6 +370,7 @@
     image_out,
     beyond_out,
     masked,
+    pair,
     send,
     scalars,
     term,
@@ -308,6 +385,8 @@
     residual_out[...] = r_next
     image_out[...] = w_next
     masked[...] = sea[...] * w_next
+    pair[0] = (sea[...] * r_next).astype(BF16)
+    pair[1] = (sea[...] * w_next).astype(BF16)
     scalars[0:1, :] = norm
     scalars[1:2, :] = step
     pack(scale[...] * w_next, r_next, w_next, send, term)
@@ -328,7 +407,6 @@
     residual_out,
     direction_out,
     along_out,
-    weights_out,
     increment_out,
     image_out,
     send,
@@ -344,7 +422,6 @@
     p = r + ratio * residual_0[...]
     s = w + ratio * image_0[...]
     z = n + ratio * beyond_0[...]
-    weights_out[...] = step_0 * residual_0[...] + step * p
     increment_out[...] = step_0 * (image_0[...] - error[...] * residual_0[...]) + step * (
         s - error[...] * p
     )
@@ -354,36 +431,30 @@
     direction_out[...] = p
     along_out[...] = s
     image_out[...] = w_next
-    scalars_out[0:1, :] = norm
-    scalars_out[1:2, :] = step
+    for i, value in enumerate((norm, step, ratio, step_0)):
+        scalars_out[i : i + 1, :] = value
     lane = lax.broadcasted_iota(jnp.int32, (1, LANES), 1)
     both = jnp.where(lane < LANES // 2, total_of(r_next * r_next), total_of(r_next * w_next))
     send[...] = jnp.broadcast_to(both[None], send.shape)
 
 
 def last_kernel(
-    got,
-    outer,
-    error,
-    residual,
-    direction,
-    along,
-    weights,
-    increment,
-    image,
-    scalars,
-    wide,
-    increment_out,
+    got, error, residual, direction, along, increment, image, scalars, factors, out
 ):
     both = jnp.sum(got[...], axis=0)
     norm, product = both[:, 0:1], both[:, LANES // 2 : LANES // 2 + 1]
-    norm_1, step_1 = scalars[0:1, 0:1], scalars[1:2, 0:1]
+    norm_1, step_1, ratio_1, step_0 = (scalars[i : i + 1, 0:1] for i in range(4))
     ratio = norm / norm_1
     step = norm / (product - ratio * norm / step_1)
     p = residual[...] + ratio * direction[...]
     s = image[...] + ratio * along[...]
-    wide[...] = (outer[...] * (weights[...] + step * p)).astype(BF16)
-    increment_out[...] = increment[...] + step * (s - error[...] * p)
+    out[...] = increment[...] + step * (s - error[...] * p)
+    held = step_1 + step * ratio
+    back = step * step_1 * ratio_1 / step_0
+    for i, value in enumerate(
+        (step_0 + held * ratio_1 - back, held + step + back, -step * step_1)
+    ):
+        factors[i : i + 1, :] = jnp.broadcast_to(value, (1, LANES))
 
 
 def kernel_call(body, arguments, outs, scratch=True):
@@ -396,11 +467,6 @@
     )(*arguments)
 
 
-def flat(values):
-    padded = jnp.pad(values, ((0, PADDED - LAYERS), (0, 0), (0, 0)))
-    return padded.reshape(FLAT, LANES)
-
-
 def exchanged(values, axes):
     return lax.all_to_all(values, axes, split_axis=0, concat_axis=0, tiled=True)
 
@@ -409,80 +475,81 @@
     count = lax.axis_size(ALL)
     place = lax.axis_index(ALL).astype(jnp.int32).reshape(1)
     vector = ((FLAT, LANES), F32)
+    rows = ((8, LANES), F32)
     packed = ((count, TILE, LANES), BF16)
+    residual, scale, sea, masked_0, halves, send = kernel_call(
+        prepare_kernel,
+        (innovations, static_scale, sea_mask),
+        (vector,) * 4 + (((2, FLAT, LANES), BF16), packed),
+    )
+    got = exchanged(send, ALL)
     blocks = to_blocks(members.reshape(members.shape[1:]))
-
-    sea = jnp.broadcast_to(sea_mask.astype(F32)[None], (PADDED, TILE, LANES)).reshape(FLAT, LANES)
-    scale = sea * flat(static_scale)
-    residual = flat(innovations)
-    source = (scale * residual).astype(BF16).reshape(PADDED, TILE, LANES)
-    send = lax.pad(
-        source,
-        jnp.zeros((), BF16),
-        ((0, count - (STRIDE * (PADDED - 1) + 1), STRIDE - 1), (0, 0, 0), (0, 0, 0)),
-    )
-    got = exchanged(send, ALL)
     tiles = exchanged(blocks, ENS_GX)
-
-    mixing = (
-        spread[:, None, :, None] * jnp.eye(TILE, dtype=spread.dtype)[None, :, None, :]
-    ).reshape(LAYERS * TILE, LAYERS * TILE)
-    mixing = jnp.pad(mixing, ((0, FLAT - LAYERS * TILE),) * 2)
-    bound = 36.0 * jnp.max(jnp.sum(jnp.abs(spread.astype(F32)), axis=1)) + 67.0
-    shrink = jnp.exp2(-jnp.ceil(jnp.log2(bound)))
-    error = shrink * flat(obs_error)
-    outer = shrink * sea
-    outer_scale = shrink * scale
+    mixing, error, outer, outer_scale, shrinks = kernel_call(
+        constants_kernel,
+        (spread, obs_error, scale, sea),
+        (((FLAT, FLAT), BF16),) + (vector,) * 3 + (rows,),
+        False,
+    )
 
     def solve(received):
-        return exchanged(whole_cycle(place, received), ALL)
-
-    solved = whole_cycle(place, got)
-    result = exchanged(solved, ALL)
-    spread_out = ensemble(tiles, sea * residual, mixing)
+        solved = whole_cycle(place, received)
+        return exchanged(solved, ALL)
+
+    def near(values):
+        return lax.all_gather(values[None], ("gx_1", "ens_0"), axis=0, tiled=True)
+
+    def far(values):
+        got = lax.all_gather(values, ("ens_1", "gx_0"), axis=0, tiled=True)
+        return got.reshape((2, 4, 4, 2) + values.shape[1:])
+
+    result = solve(got)
+    spread_out = ensemble(tiles, masked_0, mixing)
     constants = (outer, outer_scale, error)
     image, masked, send = kernel_call(
         start_kernel,
         (result, spread_out, scale, sea) + constants + (residual,),
         (vector, vector, packed),
     )
+    halves = near(halves)
+    opening = halves[:, 0].astype(F32) + halves[:, 1].astype(F32)
+    opening = (shrinks[0, 0] * opening).astype(BF16)
+    opening = far(opening)
     result = solve(exchanged(send, ALL))
     spread_out = ensemble(tiles, masked, mixing)
-    residual_1, image_1, beyond, masked, send, scalars = kernel_call(
+    residual_1, image_1, beyond, masked, pair, send, scalars = kernel_call(
         first_kernel,
         (result, spread_out, scale, sea) + constants + (residual, image),
-        (vector, vector, vector, vector, packed, ((8, LANES), F32)),
-    )
+        (vector,) * 4 + (((2, FLAT, LANES), BF16), packed, rows),
+    )
+    pair = near(pair)
+    pair = (shrinks[0, 0] * pair.astype(F32)).astype(BF16)
+    pair = far(pair)
     result = solve(exchanged(send, ALL))
     spread_out = ensemble(tiles, masked, mixing)
-    residual_2, direction, along, weights, increment, image_2, send, scalars = kernel_call(
+    residual_2, direction, along, increment, image_2, send, scalars = kernel_call(
         second_kernel,
         (result, spread_out)
         + constants
         + (residual, image, beyond, residual_1, image_1, scalars),
-        (vector,) * 6 + (((count, 1, LANES), F32), ((8, LANES), F32)),
-    )
-    wide, increment = kernel_call(
+        (vector,) * 5 + (((count, 1, LANES), F32), rows),
+    )
+    factors, increment = kernel_call(
         last_kernel,
         (
             exchanged(send, ALL),
-            outer,
             error,
             residual_2,
             direction,
             along,
-            weights,
             increment,
             image_2,
             scalars,
         ),
-        (((FLAT, LANES), BF16), vector),
+        (rows, vector),
         False,
     )
-    wide = wide[None]
-    for axes in ("gx_1", "ens_0", ("ens_1", "gx_0")):
-        wide = lax.all_gather(wide, axes, axis=0, tiled=True)
-    fields = alpha(blocks, wide.reshape(2, 4, 2, 4, FLAT, LANES), mixing)
+    fields = alpha(blocks, opening, pair, factors, mixing)
     increment = increment.reshape(PADDED, TILE, LANES)[:LAYERS]
     return increment, fields[None]
 

time: 437 us -> 409 us (0.936)
  local copies, waits for them, and re-layouts: 35.2 us -> 6.91 us
  blocking collectives: 95.8 us -> 70.7 us
  waiting for transfers between devices: 173 us -> 193 us
  Pallas kernels: 67.5 us -> 74.9 us
    all_gather x2 -> x0, blocking collectives: 23.4 us -> none  [window(): wide = lax.all_gather(wide, axes, axis=0, tiled=True)]
    pad x2 -> x0, local copies, waits for them, and re-layouts: 23.4 us -> none  [the longest x1 22.6 us: window(): lax.pad(source, jnp.zeros((), BF16), ((0, count - (STRIDE * (PADDED - 1)...]
    all_gather x1 -> x4, waiting for transfers between devices: 32.5 us -> 42.4 us  [the longest x2 28.9 us: near(): return lax.all_gather(values[None], ('gx_1', 'ens_0'), axis=0, tiled=True)]
    all_to_all x5, waiting for transfers between devices: 140 us -> 150 us  [exchanged(): return lax.all_to_all(values, axes, split_axis=0, concat_axis=0, tiled=True)]
    mul x1 -> x0, local copies, waits for them, and re-layouts: 7.15 us -> none  [window(): spread[:, None, :, None]]
    convert_element_type x2, other arithmetic: 0.69 us -> 6.17 us  [the longest x1 3.19 us: window(): pair = (shrinks[0, 0] * pair.astype(F32)).astype(BF16)]
    mul x3 -> x0, other arithmetic: 4.89 us -> none  [the longest x1 3.32 us: window(): spread[:, None, :, None]]
    pallas_call x4 -> x6, Pallas kernels: 10.3 us -> 14.7 us  [kernel_call(): pl.pallas_call(body, in_specs=[pl.BlockSpec(memory_space=pltpu.VMEM)] * l...]
  transfers between devices with their start and end apart: 6 -> 9, of which waited for: 5 -> 7; matrix products, arithmetic and copies ran while one was open for 3% -> 2% of each run, Pallas kernels for 8% -> 15%
where the time goes in v3:
time: 409 us; the launch traced here: 406 us
  waiting for transfers between devices  193 us (47%)
  Pallas kernels  74.9 us (18%)
  blocking collectives  70.7 us (17%)
  starting transfers between devices  40.7 us (10%)
  between operations  13.8 us (3%)
  local copies, waits for them, and re-layouts  6.91 us (2%)
  other arithmetic  6.17 us (2%)
    all_to_all x5, waiting for transfers between devices, exchanged(): return lax.all_to_all(values, axes, split_axis=0, concat_axis=0, tiled=True)  150 us
    all_to_all x3, blocking collectives, exchanged(): return lax.all_to_all(values, axes, split_axis=0, concat_axis=0, tiled=True)  70.7 us
    all_to_all x5, starting transfers between devices, exchanged(): return lax.all_to_all(values, axes, split_axis=0, concat_axis=0, tiled=True)  40.5 us
    all_gather x2, waiting for transfers between devices, near(): return lax.all_gather(values[None], ('gx_1', 'ens_0'), axis=0, tiled=True)  28.9 us
    pallas_call x3, Pallas kernels, ensemble(): pl.pallas_call(ensemble_kernel, grid=(members // 8,), in_specs=[pl.BlockS...  23.5 us
    pallas_call x3, Pallas kernels, whole_cycle(): pl.pallas_call(cycle_kernel, in_specs=[pl.BlockSpec(memory_space=pltpu.SM...  16.4 us
    pallas_call x6, Pallas kernels, kernel_call(): pl.pallas_call(body, in_specs=[pl.BlockSpec(memory_space=pltpu.VMEM)] * l...  14.7 us
    all_gather x2, waiting for transfers between devices, far(): got = lax.all_gather(values, ('ens_1', 'gx_0'), axis=0, tiled=True)  13.6 us
  transfers between devices with their start and end apart: 9, of which 7 were waited for; matrix products, arithmetic and copies ran while one was open for 2% of the time, Pallas kernels for 15%

profile of v3, /device:TPU:8, one launch (start us, length us, event | category | flops | bytes accessed | tf_op | source)
XLA Modules:
  0.0 406.5 jit_solution(15778620247465576800)
XLA Ops:
  7.2 2.1 shard_map.77
  9.2 14.6 %all-to-all-start = ((bf16[256,4,128]{2,1,0:T(4,128)(2,1)}), bf16[256,4,128]{2,1,0:T(4,128)(2,1)S(1)}, u32[]{:S(2)}, u32[]{:S(2)}) async-start(bf16[256,4,128]{2,1,0:T(4,128)(2,1)} %get-tuple-element.32), calls=%async_computation | async-start | bytes 524288 | tf_op jit(solution)/shard_map/all_to_all | solution.py:471
  23.8 7.6 %to_blocks.1.members = bf16[64,304,128]{2,1,0:T(8,128)(2,1)} custom-call(bf16[75,256,128]{2,1,0:T(8,128)(2,1)} %bitcast.12), custom_call_target="tpu_custom_call" | custom-call | tf_op jit(solution)/shard_map/to_blocks/pallas_call | solution.py:48
  31.5 7.4 %all-to-all-done.got = bf16[256,4,128]{2,1,0:T(4,128)(2,1)S(1)} async-done(((bf16[256,4,128]{2,1,0:T(4,128)(2,1)}), bf16[256,4,128]{2,1,0:T(4,128)(2,1)S(1)}, u32[]{:S(2)}, u32[]{:S(2)}) %all-to-all-start) | async-done | bytes 262176 | tf_op jit(solution)/shard_map/all_to_all | solution.py:471
  39.6 5.7 %all-to-all-start.2 = ((bf16[64,304,128]{2,1,0:T(8,128)(2,1)}), bf16[64,304,128]{2,1,0:T(8,128)(2,1)}, u32[]{:S(2)}, u32[]{:S(2)}) async-start(bf16[64,304,128]{2,1,0:T(8,128)(2,1)} %to_blocks.1.members), calls=%async_computation.2 | async-start | bytes 9961472 | tf_op jit(solution)/shard_map/all_to_all | solution.py:471
  45.3 5.5 %cycle.3 = f32[256,4,128]{2,1,0:T(4,128)} custom-call(s32[1]{0:T(128)} %bitcast.place, bf16[256,4,128]{2,1,0:T(4,128)(2,1)} %copy-done.3), custom_call_target="tpu_custom_call" | custom-call | flops 52428800 | bytes 786432 | tf_op jit(solution)/shard_map/cycle/pallas_call | solution.py:237
  50.7 107.8 %all-to-all-done.2.tiles = bf16[64,304,128]{2,1,0:T(8,128)(2,1)} async-done(((bf16[64,304,128]{2,1,0:T(8,128)(2,1)}), bf16[64,304,128]{2,1,0:T(8,128)(2,1)}, u32[]{:S(2)}, u32[]{:S(2)}) %all-to-all-start.2) | async-done | bytes 4980768 | tf_op jit(solution)/shard_map/all_to_all | solution.py:471
  158.5 7.2 %all-to-all-start.1 = ((f32[256,4,128]{2,1,0:T(4,128)}), f32[256,4,128]{2,1,0:T(4,128)S(1)}, u32[]{:S(2)}, u32[]{:S(2)}) async-start(f32[256,4,128]{2,1,0:T(4,128)} %cycle.3), calls=%async_computation.1 | async-start | bytes 1048576 | tf_op jit(solution)/shard_map/all_to_all | solution.py:471
  166.5 2.2 shard_map.78
  168.7 7.8 %ensemble.3.spread_out = f32[304,128]{1,0:T(8,128)} custom-call(bf16[64,304,128]{2,1,0:T(8,128)(2,1)} %all-to-all-done.2.tiles, f32[304,128]{1,0:T(8,128)} %get-tuple-element.33.vector, bf16[304,304]{1,0:T(8,128)(2,1)} %get-tuple-element.36.mixing), custom_call_target="tpu_custom_call" | custom-call | flops 1514143744 | bytes 4980736 | tf_op jit(solution)/shard_map/ensemble/pallas_call | solution.py:80
  176.5 9.7 %all-to-all-done.1.result = f32[256,4,128]{2,1,0:T(4,128)S(1)} async-done(((f32[256,4,128]{2,1,0:T(4,128)}), f32[256,4,128]{2,1,0:T(4,128)S(1)}, u32[]{:S(2)}, u32[]{:S(2)}) %all-to-all-start.1) | async-done | bytes 524320 | tf_op jit(solution)/shard_map/all_to_all | solution.py:471
  187.0 2.5 shard_map.79
  189.4 25.0 %all_to_all.40.got = bf16[256,4,128]{2,1,0:T(4,128)(2,1)} all-to-all(bf16[256,4,128]{2,1,0:T(4,128)(2,1)} %get-tuple-element.41), channel_id=1, replica_groups=mesh['ens_0'=2,'ens_1'=2,'gx_0'=4,'gx_1'=4,'gy'=4] {'ens_0','ens_1','gx_..., dimensions={0} | all-to-all | bytes 524288 | tf_op jit(solution)/shard_map/all_to_all | solution.py:471
  214.4 5.5 %cycle.4 = f32[256,4,128]{2,1,0:T(4,128)} custom-call(s32[1]{0:T(128)} %bitcast.place, bf16[256,4,128]{2,1,0:T(4,128)(2,1)} %all_to_all.40.got), custom_call_target="tpu_custom_call" | custom-call | flops 52428800 | bytes 786432 | tf_op jit(solution)/shard_map/cycle/pallas_call | solution.py:237
  219.9 6.5 %all-to-all-start.4 = ((f32[256,4,128]{2,1,0:T(4,128)}), f32[256,4,128]{2,1,0:T(4,128)S(1)}, u32[]{:S(2)}, u32[]{:S(2)}) async-start(f32[256,4,128]{2,1,0:T(4,128)} %cycle.4), calls=%async_computation.4 | async-start | bytes 1048576 | tf_op jit(solution)/shard_map/all_to_all | solution.py:471
  226.4 7.8 %ensemble.4.spread_out = f32[304,128]{1,0:T(8,128)} custom-call(bf16[64,304,128]{2,1,0:T(8,128)(2,1)} %all-to-all-done.2.tiles, f32[304,128]{1,0:T(8,128)} %get-tuple-element.42.vector, bf16[304,304]{1,0:T(8,128)(2,1)} %get-tuple-element.36.mixing), custom_call_target="tpu_custom_call" | custom-call | flops 1514143744 | bytes 4980736 | tf_op jit(solution)/shard_map/ensemble/pallas_call | solution.py:80
  234.3 12.6 %all-to-all-done.4.result = f32[256,4,128]{2,1,0:T(4,128)S(1)} async-done(((f32[256,4,128]{2,1,0:T(4,128)}), f32[256,4,128]{2,1,0:T(4,128)S(1)}, u32[]{:S(2)}, u32[]{:S(2)}) %all-to-all-start.4) | async-done | bytes 524320 | tf_op jit(solution)/shard_map/all_to_all | solution.py:471
  247.7 2.7 shard_map.80
  251.8 3.0 multiply_convert_fusion.1
  254.9 28.9 %all-gather.14.cloned.1.call-done = bf16[16,304,128]{2,1,0:T(8,128)(2,1)} async-done(((bf16[2,304,128]{2,1,0:T(8,128)(2,1)}), bf16[16,304,128]{2,1,0:T(8,128)(2,1)}) %all-gather.14.cloned.1.call-update) | async-done | bytes 1245200 | tf_op jit(solution)/shard_map/all_gather | solution.py:500
  283.7 3.2 multiply_convert_fusion
  287.9 25.3 %all_to_all.41.got = bf16[256,4,128]{2,1,0:T(4,128)(2,1)} all-to-all(bf16[256,4,128]{2,1,0:T(4,128)(2,1)S(1)} %copy-done.4), channel_id=1, replica_groups=mesh['ens_0'=2,'ens_1'=2,'gx_0'=4,'gx_1'=4,'gy'=4] {'ens_0','ens_1','gx_..., dimensions={0} | all-to-all | bytes 524288 | tf_op jit(solution)/shard_map/all_to_all | solution.py:471
  313.1 5.5 %cycle.5 = f32[256,4,128]{2,1,0:T(4,128)} custom-call(s32[1]{0:T(128)} %bitcast.place, bf16[256,4,128]{2,1,0:T(4,128)(2,1)} %all_to_all.41.got), custom_call_target="tpu_custom_call" | custom-call | flops 52428800 | bytes 786432 | tf_op jit(solution)/shard_map/cycle/pallas_call | solution.py:237
  318.6 6.5 %all-to-all-start.6 = ((f32[256,4,128]{2,1,0:T(4,128)}), f32[256,4,128]{2,1,0:T(4,128)S(1)}, u32[]{:S(2)}, u32[]{:S(2)}) async-start(f32[256,4,128]{2,1,0:T(4,128)} %cycle.5), calls=%async_computation.6 | async-start | bytes 1048576 | tf_op jit(solution)/shard_map/all_to_all | solution.py:471
  325.1 7.8 %ensemble.5.spread_out = f32[304,128]{1,0:T(8,128)} custom-call(bf16[64,304,128]{2,1,0:T(8,128)(2,1)} %all-to-all-done.2.tiles, f32[304,128]{1,0:T(8,128)} %get-tuple-element.45.vector, bf16[304,304]{1,0:T(8,128)(2,1)} %get-tuple-element.36.mixing), custom_call_target="tpu_custom_call" | custom-call | flops 1514143744 | bytes 4980736 | tf_op jit(solution)/shard_map/ensemble/pallas_call | solution.py:80
  333.0 12.7 %all-to-all-done.6.result = f32[256,4,128]{2,1,0:T(4,128)S(1)} async-done(((f32[256,4,128]{2,1,0:T(4,128)}), f32[256,4,128]{2,1,0:T(4,128)S(1)}, u32[]{:S(2)}, u32[]{:S(2)}) %all-to-all-start.6) | async-done | bytes 524320 | tf_op jit(solution)/shard_map/all_to_all | solution.py:471
  346.5 2.6 shard_map.81
  349.1 20.4 %all_to_all.42.got = f32[256,1,128]{2,1,0:T(1,128)} all-to-all(f32[256,1,128]{2,1,0:T(1,128)} %get-tuple-element.50), channel_id=1, replica_groups=mesh['ens_0'=2,'ens_1'=2,'gx_0'=4,'gx_1'=4,'gy'=4] {'ens_0','ens_1','gx_..., dimensions={0} | all-to-all | bytes 262144 | tf_op jit(solution)/shard_map/all_to_all | solution.py:471
  369.5 2.5 shard_map.82
  372.1 1.6 slice.17
  373.7 13.6 %all-gather.8.cloned.1.call-done = bf16[64,2,304,128]{3,2,1,0:T(8,128)(2,1)} async-done(((bf16[8,2,304,128]{3,2,1,0:T(8,128)(2,1)}), bf16[64,2,304,128]{3,2,1,0:T(8,128)(2,1)}) %all-gather.8.cloned.1.call-update) | async-done | bytes 9961488 | tf_op jit(solution)/shard_map/all_gather | solution.py:503
  387.3 12.7 %alpha.1 = bf16[75,256,128]{2,1,0:T(8,128)(2,1)} custom-call(bf16[64,304,128]{2,1,0:T(8,128)(2,1)} %to_blocks.1.members, bf16[2,4,4,2,304,128]{5,4,3,2,1,0:T(8,128)(2,1)} %bitcast.10, bf16[2,4,4,2,2,304,128]{6,5,4,3,2,1,0:T(8,128)(2,1)} %bitcast.9, f32[8,128]{1,0:T(8,128)} %get-tuple-element.61.coefficients, bf16[304,304]{1,0:T(8,128)(2,1)} %get-tuple-element.36.mixing), custom_call_target="tpu_custom_call" | custom-call | tf_op jit(solution)/shard_map/alpha/pallas_call | solution.py:131
  (21 shorter events, 6.2 us)
Async XLA Ops:
  9.2 29.6 %all-to-all-start = ((bf16[256,4,128]{2,1,0:T(4,128)(2,1)}), bf16[256,4,128]{2,1,0:T(4,128)(2,1)S(1)}, u32[]{:S(2)}, u32[]{:S(2)}) async-start(bf16[256,4,128]{2,1,0:T(4,128)(2,1)} %get-tuple-element.32), calls=%async_computation | async-start | bytes 524288 | tf_op jit(solution)/shard_map/all_to_all | solution.py:471
  38.9 0.7 copy-start.3
  39.6 118.9 %all-to-all-start.2 = ((bf16[64,304,128]{2,1,0:T(8,128)(2,1)}), bf16[64,304,128]{2,1,0:T(8,128)(2,1)}, u32[]{:S(2)}, u32[]{:S(2)}) async-start(bf16[64,304,128]{2,1,0:T(8,128)(2,1)} %to_blocks.1.members), calls=%async_computation.2 | async-start | bytes 9961472 | tf_op jit(solution)/shard_map/all_to_all | solution.py:471
  158.5 27.7 %all-to-all-start.1 = ((f32[256,4,128]{2,1,0:T(4,128)}), f32[256,4,128]{2,1,0:T(4,128)S(1)}, u32[]{:S(2)}, u32[]{:S(2)}) async-start(f32[256,4,128]{2,1,0:T(4,128)} %cycle.3), calls=%async_computation.1 | async-start | bytes 1048576 | tf_op jit(solution)/shard_map/all_to_all | solution.py:471
  165.7 86.1 %all-gather.10.cloned.1.call-start = ((), (), s32[]{:S(2)}) async-start(), calls=%async_computation.9 | async-start | bytes 1400832 | tf_op jit(solution)/shard_map/all_gather | solution.py:500
  186.2 0.8 copy-start
  219.9 27.0 %all-to-all-start.4 = ((f32[256,4,128]{2,1,0:T(4,128)}), f32[256,4,128]{2,1,0:T(4,128)S(1)}, u32[]{:S(2)}, u32[]{:S(2)}) async-start(f32[256,4,128]{2,1,0:T(4,128)} %cycle.4), calls=%async_computation.4 | async-start | bytes 1048576 | tf_op jit(solution)/shard_map/all_to_all | solution.py:471
  226.4 57.3 %all-gather.14.cloned.1.call-start = ((), (), s32[]{:S(2)}) async-start(), calls=%async_computation.11 | async-start | bytes 1400832 | tf_op jit(solution)/shard_map/all_gather | solution.py:500
  246.9 0.8 copy-start.1
  250.5 123.2 %all-gather.12.cloned.1.call-start = ((), (), s32[]{:S(2)}) async-start(), calls=%async_computation.10 | async-start | bytes 5603328 | tf_op jit(solution)/shard_map/all_gather | solution.py:503
  254.8 132.4 %all-gather.8.cloned.1.call-start = ((), (), s32[]{:S(2)}) async-start(), calls=%async_computation.8 | async-start | bytes 11206656 | tf_op jit(solution)/shard_map/all_gather | solution.py:503
  286.9 0.9 copy-start.4
  318.6 27.0 %all-to-all-start.6 = ((f32[256,4,128]{2,1,0:T(4,128)}), f32[256,4,128]{2,1,0:T(4,128)S(1)}, u32[]{:S(2)}, u32[]{:S(2)}) async-start(f32[256,4,128]{2,1,0:T(4,128)} %cycle.5), calls=%async_computation.6 | async-start | bytes 1048576 | tf_op jit(solution)/shard_map/all_to_all | solution.py:471
  345.7 0.8 copy-start.2
Sparse Core Ops, SparseCore 0:
  168.3 43.3 all-gather.9
  250.6 33.0 all-gather.13
  285.6 39.2 all-gather.11
  327.2 60.0 all-gather.7

commit v4 on v3

--- a/solution.py
+++ b/solution.py
@@ -17,6 +17,7 @@
 FLAT = PADDED * TILE
 LANES = 128
 STRIDE = 3
+HALF = TILE // 2
 F32 = jnp.float32
 BF16 = jnp.bfloat16
 
@@ -221,9 +222,13 @@
             rows, columns = TILE * (slot // 4), LANES * (slot % 4)
             grid[rows : rows + TILE, columns : columns + LANES] = got[slot].astype(F32)
         grid[...] = cycle(grid[...], 0)
-        for slot in range(count):
-            rows, columns = TILE * (slot // 4), LANES * (slot % 4)
-            out[slot] = grid[rows : rows + TILE, columns : columns + LANES]
+        for half in range(2):
+
+            @pl.when((place[0] % STRIDE == 1) == (half == 1))
+            def _():
+                for slot in range(count):
+                    rows, columns = TILE * (slot // 4) + HALF * half, LANES * (slot % 4)
+                    out[slot] = grid[rows : rows + HALF, columns : columns + LANES]
 
     @pl.when(place[0] >= count - 2)
     def _():
@@ -241,7 +246,7 @@
             pl.BlockSpec(memory_space=pltpu.VMEM),
         ],
         out_specs=pl.BlockSpec(memory_space=pltpu.VMEM),
-        out_shape=jax.ShapeDtypeStruct(got.shape, F32),
+        out_shape=jax.ShapeDtypeStruct((count, HALF, LANES), F32),
         scratch_shapes=[pltpu.VMEM((count, 4 * LANES), F32)],
         cost_estimate=pl.CostEstimate(
             flops=400 * count * 4 * LANES, transcendentals=0, bytes_accessed=6 * got.size
@@ -256,14 +261,18 @@
 
 def unpack(result, term):
     for layer in range(PADDED):
-        term[TILE * layer : TILE * (layer + 1), :] = result[STRIDE * layer]
+        for half in range(2):
+            row = TILE * layer + HALF * half
+            term[row : row + HALF, :] = result[STRIDE * layer + half]
 
 
 def pack(source, residual, image, send, term):
     term[...] = source
     send[...] = jnp.zeros(send.shape, BF16)
     for layer in range(PADDED):
-        send[STRIDE * layer] = term[TILE * layer : TILE * (layer + 1), :].astype(BF16)
+        tile = term[TILE * layer : TILE * (layer + 1), :].astype(BF16)
+        send[STRIDE * layer] = tile
+        send[STRIDE * layer + 1] = tile
     for slot, values in ((2, residual * residual), (1, residual * image)):
         left = jnp.sum(values, axis=0, keepdims=True)
         for part in range(3):
@@ -294,7 +303,9 @@
     term[...] = scale[...] * r
     send[...] = jnp.zeros(send.shape, BF16)
     for layer in range(PADDED):
-        send[STRIDE * layer] = term[TILE * layer : TILE * (layer + 1), :].astype(BF16)
+        tile = term[TILE * layer : TILE * (layer + 1), :].astype(BF16)
+        send[STRIDE * layer] = tile
+        send[STRIDE * layer + 1] = tile
 
 
 def constants_kernel(spread, obs_error, scale, sea, mixing, error, outer, outer_scale, shrinks):

time: 409 us -> 409 us (level)
    all_gather x2, waiting for transfers between devices: 13.6 us -> 19.2 us  [far(): got = lax.all_gather(values, ('ens_1', 'gx_0'), axis=0, tiled=True)]
    all_to_all x5, waiting for transfers between devices: 150 us -> 145 us  [exchanged(): return lax.all_to_all(values, axes, split_axis=0, concat_axis=0, tiled=True)]
where the time goes in v4:
time: 409 us; the launch traced here: 407 us
  waiting for transfers between devices  195 us (48%)
  Pallas kernels  74.9 us (18%)
  blocking collectives  69.4 us (17%)
  starting transfers between devices  40.6 us (10%)
  between operations  13.8 us (3%)
  local copies, waits for them, and re-layouts  6.64 us (2%)
  other arithmetic  6.31 us (2%)
    all_to_all x5, waiting for transfers between devices, exchanged(): return lax.all_to_all(values, axes, split_axis=0, concat_axis=0, tiled=True)  145 us
    all_to_all x3, blocking collectives, exchanged(): return lax.all_to_all(values, axes, split_axis=0, concat_axis=0, tiled=True)  69.4 us
    all_to_all x5, starting transfers between devices, exchanged(): return lax.all_to_all(values, axes, split_axis=0, concat_axis=0, tiled=True)  40.5 us
    all_gather x2, waiting for transfers between devices, near(): return lax.all_gather(values[None], ('gx_1', 'ens_0'), axis=0, tiled=True)  29.5 us
    pallas_call x3, Pallas kernels, ensemble(): pl.pallas_call(ensemble_kernel, grid=(members // 8,), in_specs=[pl.BlockS...  23.5 us
    all_gather x2, waiting for transfers between devices, far(): got = lax.all_gather(values, ('ens_1', 'gx_0'), axis=0, tiled=True)  19.2 us
    pallas_call x3, Pallas kernels, whole_cycle(): pl.pallas_call(cycle_kernel, in_specs=[pl.BlockSpec(memory_space=pltpu.SM...  16.4 us
    pallas_call x6, Pallas kernels, kernel_call(): pl.pallas_call(body, in_specs=[pl.BlockSpec(memory_space=pltpu.VMEM)] * l...  14.7 us
  transfers between devices with their start and end apart: 9, of which 7 were waited for; matrix products, arithmetic and copies ran while one was open for 2% of the time, Pallas kernels for 15%

profile of v4, /device:TPU:8, one launch (start us, length us, event | category | flops | bytes accessed | tf_op | source)
XLA Modules:
  0.0 406.6 jit_solution(18174603173212481836)
XLA Ops:
  7.2 2.1 shard_map.77
  9.2 14.6 %all-to-all-start = ((bf16[256,4,128]{2,1,0:T(4,128)(2,1)}), bf16[256,4,128]{2,1,0:T(4,128)(2,1)S(1)}, u32[]{:S(2)}, u32[]{:S(2)}) async-start(bf16[256,4,128]{2,1,0:T(4,128)(2,1)} %get-tuple-element.32), calls=%async_computation | async-start | bytes 524288 | tf_op jit(solution)/shard_map/all_to_all | solution.py:482
  23.8 7.6 %to_blocks.1.members = bf16[64,304,128]{2,1,0:T(8,128)(2,1)} custom-call(bf16[75,256,128]{2,1,0:T(8,128)(2,1)} %bitcast.12), custom_call_target="tpu_custom_call" | custom-call | tf_op jit(solution)/shard_map/to_blocks/pallas_call | solution.py:49
  31.5 7.4 %all-to-all-done.got = bf16[256,4,128]{2,1,0:T(4,128)(2,1)S(1)} async-done(((bf16[256,4,128]{2,1,0:T(4,128)(2,1)}), bf16[256,4,128]{2,1,0:T(4,128)(2,1)S(1)}, u32[]{:S(2)}, u32[]{:S(2)}) %all-to-all-start) | async-done | bytes 262176 | tf_op jit(solution)/shard_map/all_to_all | solution.py:482
  39.6 5.7 %all-to-all-start.2 = ((bf16[64,304,128]{2,1,0:T(8,128)(2,1)}), bf16[64,304,128]{2,1,0:T(8,128)(2,1)}, u32[]{:S(2)}, u32[]{:S(2)}) async-start(bf16[64,304,128]{2,1,0:T(8,128)(2,1)} %to_blocks.1.members), calls=%async_computation.2 | async-start | bytes 9961472 | tf_op jit(solution)/shard_map/all_to_all | solution.py:482
  46.0 5.4 %cycle.3 = f32[256,2,128]{2,1,0:T(2,128)} custom-call(s32[1]{0:T(128)} %bitcast.place, bf16[256,4,128]{2,1,0:T(4,128)(2,1)} %copy-done.1), custom_call_target="tpu_custom_call" | custom-call | flops 52428800 | bytes 786432 | tf_op jit(solution)/shard_map/cycle/pallas_call | solution.py:242
  51.4 118.7 %all-to-all-done.2.tiles = bf16[64,304,128]{2,1,0:T(8,128)(2,1)} async-done(((bf16[64,304,128]{2,1,0:T(8,128)(2,1)}), bf16[64,304,128]{2,1,0:T(8,128)(2,1)}, u32[]{:S(2)}, u32[]{:S(2)}) %all-to-all-start.2) | async-done | bytes 4980768 | tf_op jit(solution)/shard_map/all_to_all | solution.py:482
  170.1 7.3 %all-to-all-start.1 = ((f32[256,2,128]{2,1,0:T(2,128)}), f32[256,2,128]{2,1,0:T(2,128)S(1)}, u32[]{:S(2)}, u32[]{:S(2)}) async-start(f32[256,2,128]{2,1,0:T(2,128)} %cycle.3), calls=%async_computation.1 | async-start | bytes 524288 | tf_op jit(solution)/shard_map/all_to_all | solution.py:482
  177.4 2.2 shard_map.78
  179.6 7.8 %ensemble.3.spread_out = f32[304,128]{1,0:T(8,128)} custom-call(bf16[64,304,128]{2,1,0:T(8,128)(2,1)} %all-to-all-done.2.tiles, f32[304,128]{1,0:T(8,128)} %get-tuple-element.33.vector, bf16[304,304]{1,0:T(8,128)(2,1)} %get-tuple-element.36.mixing), custom_call_target="tpu_custom_call" | custom-call | flops 1514143744 | bytes 4980736 | tf_op jit(solution)/shard_map/ensemble/pallas_call | solution.py:81
  187.4 5.0 %all-to-all-done.1.result = f32[256,2,128]{2,1,0:T(2,128)S(1)} async-done(((f32[256,2,128]{2,1,0:T(2,128)}), f32[256,2,128]{2,1,0:T(2,128)S(1)}, u32[]{:S(2)}, u32[]{:S(2)}) %all-to-all-start.1) | async-done | bytes 262176 | tf_op jit(solution)/shard_map/all_to_all | solution.py:482
  193.1 2.4 shard_map.79
  195.5 23.9 %all_to_all.40.got = bf16[256,4,128]{2,1,0:T(4,128)(2,1)} all-to-all(bf16[256,4,128]{2,1,0:T(4,128)(2,1)} %get-tuple-element.41), channel_id=1, replica_groups=mesh['ens_0'=2,'ens_1'=2,'gx_0'=4,'gx_1'=4,'gy'=4] {'ens_0','ens_1','gx_..., dimensions={0} | all-to-all | bytes 524288 | tf_op jit(solution)/shard_map/all_to_all | solution.py:482
  219.4 5.6 %cycle.4 = f32[256,2,128]{2,1,0:T(2,128)} custom-call(s32[1]{0:T(128)} %bitcast.place, bf16[256,4,128]{2,1,0:T(4,128)(2,1)} %all_to_all.40.got), custom_call_target="tpu_custom_call" | custom-call | flops 52428800 | bytes 786432 | tf_op jit(solution)/shard_map/cycle/pallas_call | solution.py:242
  224.9 6.5 %all-to-all-start.4 = ((f32[256,2,128]{2,1,0:T(2,128)}), f32[256,2,128]{2,1,0:T(2,128)S(1)}, u32[]{:S(2)}, u32[]{:S(2)}) async-start(f32[256,2,128]{2,1,0:T(2,128)} %cycle.4), calls=%async_computation.4 | async-start | bytes 524288 | tf_op jit(solution)/shard_map/all_to_all | solution.py:482
  231.5 7.8 %ensemble.4.spread_out = f32[304,128]{1,0:T(8,128)} custom-call(bf16[64,304,128]{2,1,0:T(8,128)(2,1)} %all-to-all-done.2.tiles, f32[304,128]{1,0:T(8,128)} %get-tuple-element.42.vector, bf16[304,304]{1,0:T(8,128)(2,1)} %get-tuple-element.36.mixing), custom_call_target="tpu_custom_call" | custom-call | flops 1514143744 | bytes 4980736 | tf_op jit(solution)/shard_map/ensemble/pallas_call | solution.py:81
  239.3 7.2 %all-to-all-done.4.result = f32[256,2,128]{2,1,0:T(2,128)S(1)} async-done(((f32[256,2,128]{2,1,0:T(2,128)}), f32[256,2,128]{2,1,0:T(2,128)S(1)}, u32[]{:S(2)}, u32[]{:S(2)}) %all-to-all-start.4) | async-done | bytes 262176 | tf_op jit(solution)/shard_map/all_to_all | solution.py:482
  247.3 2.6 shard_map.80
  251.2 3.1 multiply_convert_fusion.1
  254.3 29.5 %all-gather.14.cloned.1.call-done = bf16[16,304,128]{2,1,0:T(8,128)(2,1)} async-done(((bf16[2,304,128]{2,1,0:T(8,128)(2,1)}), bf16[16,304,128]{2,1,0:T(8,128)(2,1)}) %all-gather.14.cloned.1.call-update) | async-done | bytes 1245200 | tf_op jit(solution)/shard_map/all_gather | solution.py:511
  283.8 3.3 multiply_convert_fusion
  288.0 25.3 %all_to_all.41.got = bf16[256,4,128]{2,1,0:T(4,128)(2,1)} all-to-all(bf16[256,4,128]{2,1,0:T(4,128)(2,1)S(1)} %copy-done.4), channel_id=1, replica_groups=mesh['ens_0'=2,'ens_1'=2,'gx_0'=4,'gx_1'=4,'gy'=4] {'ens_0','ens_1','gx_..., dimensions={0} | all-to-all | bytes 524288 | tf_op jit(solution)/shard_map/all_to_all | solution.py:482
  313.3 5.4 %cycle.5 = f32[256,2,128]{2,1,0:T(2,128)} custom-call(s32[1]{0:T(128)} %bitcast.place, bf16[256,4,128]{2,1,0:T(4,128)(2,1)} %all_to_all.41.got), custom_call_target="tpu_custom_call" | custom-call | flops 52428800 | bytes 786432 | tf_op jit(solution)/shard_map/cycle/pallas_call | solution.py:242
  318.7 6.4 %all-to-all-start.6 = ((f32[256,2,128]{2,1,0:T(2,128)}), f32[256,2,128]{2,1,0:T(2,128)S(1)}, u32[]{:S(2)}, u32[]{:S(2)}) async-start(f32[256,2,128]{2,1,0:T(2,128)} %cycle.5), calls=%async_computation.6 | async-start | bytes 524288 | tf_op jit(solution)/shard_map/all_to_all | solution.py:482
  325.1 7.8 %ensemble.5.spread_out = f32[304,128]{1,0:T(8,128)} custom-call(bf16[64,304,128]{2,1,0:T(8,128)(2,1)} %all-to-all-done.2.tiles, f32[304,128]{1,0:T(8,128)} %get-tuple-element.45.vector, bf16[304,304]{1,0:T(8,128)(2,1)} %get-tuple-element.36.mixing), custom_call_target="tpu_custom_call" | custom-call | flops 1514143744 | bytes 4980736 | tf_op jit(solution)/shard_map/ensemble/pallas_call | solution.py:81
  332.9 7.2 %all-to-all-done.6.result = f32[256,2,128]{2,1,0:T(2,128)S(1)} async-done(((f32[256,2,128]{2,1,0:T(2,128)}), f32[256,2,128]{2,1,0:T(2,128)S(1)}, u32[]{:S(2)}, u32[]{:S(2)}) %all-to-all-start.6) | async-done | bytes 262176 | tf_op jit(solution)/shard_map/all_to_all | solution.py:482
  340.9 3.0 shard_map.81
  343.8 20.3 %all_to_all.42.got = f32[256,1,128]{2,1,0:T(1,128)} all-to-all(f32[256,1,128]{2,1,0:T(1,128)} %get-tuple-element.50), channel_id=1, replica_groups=mesh['ens_0'=2,'ens_1'=2,'gx_0'=4,'gx_1'=4,'gy'=4] {'ens_0','ens_1','gx_..., dimensions={0} | all-to-all | bytes 262144 | tf_op jit(solution)/shard_map/all_to_all | solution.py:482
  364.1 2.5 shard_map.82
  366.6 1.6 slice.17
  368.2 19.2 %all-gather.8.cloned.1.call-done = bf16[64,2,304,128]{3,2,1,0:T(8,128)(2,1)} async-done(((bf16[8,2,304,128]{3,2,1,0:T(8,128)(2,1)}), bf16[64,2,304,128]{3,2,1,0:T(8,128)(2,1)}) %all-gather.8.cloned.1.call-update) | async-done | bytes 9961488 | tf_op jit(solution)/shard_map/all_gather | solution.py:514
  387.3 12.7 %alpha.1 = bf16[75,256,128]{2,1,0:T(8,128)(2,1)} custom-call(bf16[64,304,128]{2,1,0:T(8,128)(2,1)} %to_blocks.1.members, bf16[2,4,4,2,304,128]{5,4,3,2,1,0:T(8,128)(2,1)} %bitcast.10, bf16[2,4,4,2,2,304,128]{6,5,4,3,2,1,0:T(8,128)(2,1)} %bitcast.9, f32[8,128]{1,0:T(8,128)} %get-tuple-element.61.coefficients, bf16[304,304]{1,0:T(8,128)(2,1)} %get-tuple-element.36.mixing), custom_call_target="tpu_custom_call" | custom-call | tf_op jit(solution)/shard_map/alpha/pallas_call | solution.py:132
  (21 shorter events, 5.9 us)
Async XLA Ops:
  9.2 29.6 %all-to-all-start = ((bf16[256,4,128]{2,1,0:T(4,128)(2,1)}), bf16[256,4,128]{2,1,0:T(4,128)(2,1)S(1)}, u32[]{:S(2)}, u32[]{:S(2)}) async-start(bf16[256,4,128]{2,1,0:T(4,128)(2,1)} %get-tuple-element.32), calls=%async_computation | async-start | bytes 524288 | tf_op jit(solution)/shard_map/all_to_all | solution.py:482
  38.9 0.7 copy-start.1
  39.6 130.5 %all-to-all-start.2 = ((bf16[64,304,128]{2,1,0:T(8,128)(2,1)}), bf16[64,304,128]{2,1,0:T(8,128)(2,1)}, u32[]{:S(2)}, u32[]{:S(2)}) async-start(bf16[64,304,128]{2,1,0:T(8,128)(2,1)} %to_blocks.1.members), calls=%async_computation.2 | async-start | bytes 9961472 | tf_op jit(solution)/shard_map/all_to_all | solution.py:482
  45.3 205.9 %all-gather.10.cloned.1.call-start = ((), (), s32[]{:S(2)}) async-start(), calls=%async_computation.9 | async-start | bytes 1400832 | tf_op jit(solution)/shard_map/all_gather | solution.py:511
  170.1 22.3 %all-to-all-start.1 = ((f32[256,2,128]{2,1,0:T(2,128)}), f32[256,2,128]{2,1,0:T(2,128)S(1)}, u32[]{:S(2)}, u32[]{:S(2)}) async-start(f32[256,2,128]{2,1,0:T(2,128)} %cycle.3), calls=%async_computation.1 | async-start | bytes 524288 | tf_op jit(solution)/shard_map/all_to_all | solution.py:482
  192.4 0.7 copy-start.3
  224.9 21.6 %all-to-all-start.4 = ((f32[256,2,128]{2,1,0:T(2,128)}), f32[256,2,128]{2,1,0:T(2,128)S(1)}, u32[]{:S(2)}, u32[]{:S(2)}) async-start(f32[256,2,128]{2,1,0:T(2,128)} %cycle.4), calls=%async_computation.4 | async-start | bytes 524288 | tf_op jit(solution)/shard_map/all_to_all | solution.py:482
  231.4 52.4 %all-gather.14.cloned.1.call-start = ((), (), s32[]{:S(2)}) async-start(), calls=%async_computation.11 | async-start | bytes 1400832 | tf_op jit(solution)/shard_map/all_gather | solution.py:511
  246.5 0.7 copy-start.2
  249.9 118.3 %all-gather.12.cloned.1.call-start = ((), (), s32[]{:S(2)}) async-start(), calls=%async_computation.10 | async-start | bytes 5603328 | tf_op jit(solution)/shard_map/all_gather | solution.py:514
  254.3 133.1 %all-gather.8.cloned.1.call-start = ((), (), s32[]{:S(2)}) async-start(), calls=%async_computation.8 | async-start | bytes 11206656 | tf_op jit(solution)/shard_map/all_gather | solution.py:514
  287.1 0.9 copy-start.4
  318.7 21.4 %all-to-all-start.6 = ((f32[256,2,128]{2,1,0:T(2,128)}), f32[256,2,128]{2,1,0:T(2,128)S(1)}, u32[]{:S(2)}, u32[]{:S(2)}) async-start(f32[256,2,128]{2,1,0:T(2,128)} %cycle.5), calls=%async_computation.6 | async-start | bytes 524288 | tf_op jit(solution)/shard_map/all_to_all | solution.py:482
  340.1 0.7 copy-start
Sparse Core Ops, SparseCore 0:
  47.9 59.4 all-gather.9
  250.0 33.7 all-gather.13
  285.7 39.2 all-gather.11
  327.3 60.0 all-gather.7
